TPU v7x, 768 devices: a whole 4x8x12 slice. The times are simulated.
768 devices in a mesh: blk: 384 (over y, x, z), rep: 2 (over core).
Axes of the slice: x: 4, y: 8, z: 12, core: 2. Of those that a mesh axis runs over, the one named last changes fastest.
Arguments:
- star_pos: float32 [3, 98304], P(None, 'blk'), may hold values from -6 to 6
- star_vel: float32 [3, 98304], P(None, 'blk'), may hold values from -3 to 3
- star_acc: float32 [3, 98304], P(None, 'blk'), may hold values from -3 to 3
- star_jerk: float32 [3, 98304], P(None, 'blk'), may hold values from -6 to 6
- masses: float32 [98304], P('blk'), may hold values from 5.086263e-06 to 2.0345053e-05
- act_index: int32 [384, 16], P('blk'), may hold values from 0 to 255, as said below
- act_count: int32 [384], replicated, may hold values from 1 to 16, 3072 in all
Outputs:
- new_pos: float32 [3, 98304], P(None, 'blk')
- new_vel: float32 [3, 98304], P(None, 'blk')
- new_acc: float32 [3, 98304], P(None, 'blk')
- new_jerk: float32 [3, 98304], P(None, 'blk')
Inputs may be any that keep to these rules, and one draw needn't show every extreme that they name: `act_index`: within a row all 16 entries differ. `act_count`: the counts sum to 3072, and the largest equals 16.
All inputs are finite; a program needn't handle non-finite values.
Results may differ from a plain program's by a relative error of at most 0.00024.
Values sent between devices are 32-bit elements; how exact they have to be, the bound alone decides.
No kernel may reach another device: no remote copies, remote signals or barrier semaphores. Data moves between devices by JAX's collectives and lax.ppermute only.
A program may use at most 32 MiB of HBM per device.

v0:
```python
import jax
import jax.numpy as jnp
from jax import lax
from jax.sharding import Mesh
from jax.sharding import PartitionSpec as P

BLK = ("blk_0", "blk_1", "blk_2")


STEP_TIME = 0.0625
SOFTEN_SQ = 0.0001


def in_order(tiles, dim):
    shape = list(tiles.shape[1:])
    shape[dim] *= tiles.shape[0]
    return jnp.moveaxis(tiles, 0, dim).reshape(shape)


def gather_in_order(value, axes, order):
    tiles = value
    for k in order:
        tiles = lax.all_gather(tiles, axes[k])
    done = order[::-1]
    back = [done.index(k) for k in range(len(axes))]
    tiles = tiles.transpose(*back, *range(len(axes), tiles.ndim))
    return tiles.reshape(-1, *value.shape)


def gathered_by_axis(value, axes, order, dim):
    return in_order(gather_in_order(value, axes, order), dim)


def scatter_axes(value, axes, dim):
    for axis in axes:
        value = lax.psum_scatter(value, axis, scatter_dimension=dim, tiled=True)
    return value


def predict(position, velocity, accel, jerk_old):
    half_sq = STEP_TIME * STEP_TIME / 2.0
    pred_pos = (
        position + STEP_TIME * velocity + half_sq * accel + STEP_TIME * half_sq / 3.0 * jerk_old
    )
    pred_vel = velocity + STEP_TIME * accel + half_sq * jerk_old
    return (pred_pos, pred_vel)


def pair_forces(active, field, tile_cap):
    count_cols = active.shape[1]
    tile_width = tile_cap
    while count_cols % tile_width != 0:
        tile_width = tile_width // 2
    blocks = active.reshape(6, count_cols // tile_width, tile_width).transpose(1, 0, 2)

    def one_block(block):
        delta_x = field[0][None, :] - block[0][:, None]
        delta_y = field[1][None, :] - block[1][:, None]
        delta_z = field[2][None, :] - block[2][:, None]
        delta_u = field[3][None, :] - block[3][:, None]
        delta_v = field[4][None, :] - block[4][:, None]
        delta_w = field[5][None, :] - block[5][:, None]
        radius_sq = delta_x * delta_x + delta_y * delta_y + delta_z * delta_z + SOFTEN_SQ
        inverse = 1.0 / radius_sq
        weight = field[6][None, :] * inverse * jnp.sqrt(inverse)
        radial = 3.0 * (delta_x * delta_u + delta_y * delta_v + delta_z * delta_w) * inverse
        return jnp.stack(
            [
                jnp.sum(weight * delta_x, axis=1),
                jnp.sum(weight * delta_y, axis=1),
                jnp.sum(weight * delta_z, axis=1),
                jnp.sum(weight * (delta_u - radial * delta_x), axis=1),
                jnp.sum(weight * (delta_v - radial * delta_y), axis=1),
                jnp.sum(weight * (delta_w - radial * delta_z), axis=1),
            ]
        )

    result = lax.map(one_block, blocks)
    return result.transpose(1, 0, 2).reshape(6, count_cols)


def correct(state_old, forces):
    pos_zero = state_old[0:3]
    vel_zero = state_old[3:6]
    acc_zero = state_old[6:9]
    jerk_zero = state_old[9:12]
    acc_one = forces[0:3]
    jerk_one = forces[3:6]
    vel_one = (
        vel_zero
        + (acc_zero + acc_one) * (STEP_TIME / 2.0)
        + (jerk_zero - jerk_one) * (STEP_TIME * STEP_TIME / 12.0)
    )
    pos_one = (
        pos_zero
        + (vel_zero + vel_one) * (STEP_TIME / 2.0)
        + (acc_zero - acc_one) * (STEP_TIME * STEP_TIME / 12.0)
    )
    return jnp.concatenate([pos_one, vel_one, acc_one, jerk_one], axis=0)


def shards(star_pos, star_vel, star_acc, star_jerk, masses, act_index, act_count):
    shard_here = lax.axis_index(BLK)
    replica = lax.axis_index("rep")
    slot_total = act_index.shape[1]
    half_slots = slot_total // 2
    pred_pos, pred_vel = predict(star_pos, star_vel, star_acc, star_jerk)
    field = jnp.concatenate([pred_pos, pred_vel, masses[None, :]], axis=0)
    row_index = act_index[0]
    half_index = lax.dynamic_slice_in_dim(row_index, replica * half_slots, half_slots)
    act_block = field[0:6][:, half_index]
    partial_value = pair_forces(gathered_by_axis(act_block, BLK, (0, 2, 1), 1), field, 512)
    forces = scatter_axes(partial_value, BLK, 1)
    state = jnp.concatenate([star_pos, star_vel, star_acc, star_jerk], axis=0)
    updated = correct(state[:, half_index], forces)
    both_halves = lax.all_gather(updated, "rep", axis=1, tiled=True)
    count_here = lax.dynamic_index_in_dim(act_count, shard_here, keepdims=False)
    live_slots = jnp.arange(slot_total, dtype=jnp.int32) < count_here
    previous = state[:, row_index]
    state = state.at[:, row_index].set(jnp.where(live_slots[None, :], both_halves, previous))
    return (state[0:3], state[3:6], state[6:9], state[9:12])


def solution(mesh):
    finer = Mesh(
        mesh.devices.reshape(8, 4, 12, mesh.shape["rep"]), ("blk_0", "blk_1", "blk_2", "rep")
    )
    placed = (P(None, BLK), P(None, BLK), P(None, BLK), P(None, BLK), P(BLK), P(BLK, None), P())
    return jax.shard_map(
        shards,
        mesh=finer,
        in_specs=placed,
        out_specs=(P(None, BLK), P(None, BLK), P(None, BLK), P(None, BLK)),
        check_vma=False,
    )
```

profile of v0, /device:TPU:1, one launch (start us, length us, event | category | flops | bytes accessed | tf_op | source)
XLA Modules:
  0.0 226.8 jit_solution(5962997548223678605)
XLA Ops:
  7.2 0.7 fusion.21
  8.0 0.7 multiply_add_fusion.2
  9.5 20.7 %all-gather.3 = f32[8,6,8]{2,1,0:T(8,128)S(1)} all-gather(f32[1,6,8]{2,1,0:T(8,128)S(1)} %bitcast.131), channel_id=2, replica_groups=mesh['blk_0'=8,'blk_1'=4,'blk_2'=12,'rep'=2] {'blk_0'}, dimensions={0}, use_global_device_ids=true | all-gather | bytes 1728 | tf_op jit(solution)/shard_map/all_gather | solution.py:23
  30.2 28.3 %all-gather.1 = f32[96,6,8]{2,0,1:T(8,128)S(1)} all-gather(f32[8,6,8]{2,0,1:T(8,128)S(1)} %copy.80), channel_id=3, replica_groups=mesh['blk_0'=8,'blk_1'=4,'blk_2'=12,'rep'=2] {'blk_2'}, dimensions={0}, use_global_device_ids=true | all-gather | bytes 19968 | tf_op jit(solution)/shard_map/all_gather | solution.py:23
  58.6 12.1 %all-gather.2 = f32[48,8,6,8]{3,1,2,0:T(8,128)S(1)} all-gather(f32[12,8,6,8]{3,1,2,0:T(8,128)S(1)} %copy.81), channel_id=4, replica_groups=mesh['blk_0'=8,'blk_1'=4,'blk_2'=12,'rep'=2] {'blk_1'}, dimensions={0}, use_global_device_ids=true | all-gather | bytes 92160 | tf_op jit(solution)/shard_map/all_gather | solution.py:23
  70.7 1.4 copy.82
  72.1 0.7 reshape.93
  73.8 9.7 %while.10 = (s32[]{:T(128)}, f32[6,6,512]{2,1,0:T(8,128)S(1)}, f32[1,256]{1,0:T(1,128)S(1)}, f32[3,256]{1,0:T(4,128)S(1)}, f32[6,6,512]{2,0,1:T(8,128)S(1)}, /*i...) while((s32[]{:T(128)}, f32[6,6,512]{2,1,0:T(8,128)S(1)}, ...), condition=%wide.region_7.8_spmd, body=%wide.region_0.7_spmd.sunk | while | flops 5239815 | bytes 126165 | solution.py:78
  73.9 1.5 fusion.29
  75.5 1.5 fusion.29
  77.1 1.5 fusion.29
  78.7 1.5 fusion.29
  80.3 1.5 fusion.29
  81.9 1.5 fusion.29
  83.5 1.7 copy.85
  85.9 1.3 dynamic_slice.13
  87.2 46.8 %reduce-scatter.3.cloned.1.call-done = f32[6,384]{0,1:T(8,128)} async-done(((f32[6,3072]{0,1:T(8,128)}), f32[6,384]{0,1:T(8,128)}) %reduce-scatter.3.cloned.1.call-update) | async-done | bytes 9232 | tf_op jit(solution)/shard_map/reduce_scatter | solution.py:36
  135.3 1.3 dynamic-slice.1
  137.2 29.7 %reduce-scatter.5.cloned.1.call-done = f32[6,96]{0,1:T(8,128)} async-done(((f32[6,384]{0,1:T(8,128)}), f32[6,96]{0,1:T(8,128)}) %reduce-scatter.5.cloned.1.call-update) | async-done | bytes 2320 | tf_op jit(solution)/shard_map/reduce_scatter | solution.py:36
  167.0 34.5 %all-reduce = f32[6,96]{0,1:T(8,128)S(1)} all-reduce(f32[6,96]{0,1:T(8,128)} %reduce-scatter.5.cloned.1.call-done), channel_id=7, replica_groups=mesh['blk_0'=8,'blk_1'=4,'blk_2'=12,'rep'=2] {'blk_2'}, use_global_device_ids=true, to_apply=%region_10.11.clone | all-reduce | flops 576 | bytes 4608
  201.7 14.7 %all_gather.27 = f32[12,16]{0,1:T(8,128)S(1)} all-gather(f32[12,8]{0,1:T(8,128)S(1)} %pad_maximum_fusion.2), channel_id=1, replica_groups=mesh['blk_0'=8,'blk_1'=4,'blk_2'=12,'rep'=2] {'rep'}, dimensions={1}, use_global_device_ids=true | all-gather | bytes 1152 | tf_op jit(solution)/shard_map/all_gather | solution.py:116
  216.3 0.8 scatter_custom_fusion
  217.3 0.7 copy.88
  217.9 0.7 copy.89
  (62 shorter events, 5.9 us)
Async XLA Ops:
  7.2 126.8 %reduce-scatter.3.cloned.1.call-start = ((), (), s32[]{:S(2)}) async-start(), calls=%async_computation.2 | async-start | bytes 1769472 | tf_op jit(solution)/shard_map/reduce_scatter | solution.py:36
  72.8 1.0 copy-start.4
  85.2 0.7 copy-start.5
  85.2 2.0 copy-start
  85.2 2.0 copy-start.1
  85.2 2.0 copy-start.2
  85.2 2.0 copy-start.3
  85.2 81.8 %reduce-scatter.5.cloned.1.call-start = ((), (), s32[]{:S(2)}) async-start(), calls=%async_computation.3 | async-start | bytes 245760 | tf_op jit(solution)/shard_map/reduce_scatter | solution.py:36
Sparse Core Ops, SparseCore 0:
  85.3 48.5 reduce-scatter.2
  137.0 29.9 reduce-scatter.4
where the time goes:
time: 227 us
  blocking collectives  110 us (48%)
  waiting for transfers between devices  76.6 us (34%)
  between operations  14.9 us (7%)
  local copies, waits for them, and re-layouts  12.6 us (6%)
  other arithmetic  12.1 us (5%)
    reduce_scatter x2, waiting for transfers between devices, scatter_axes(): value = lax.psum_scatter(value, axis, scatter_dimension=dim, tiled=True)  76.5 us
    all_gather x3, blocking collectives, gather_in_order(): tiles = lax.all_gather(tiles, axes[k])  61.1 us
    unnamed x1, blocking collectives  34.5 us
    all_gather x1, blocking collectives, shards(): both_halves = lax.all_gather(updated, 'rep', axis=1, tiled=True)  14.7 us
    reduce_sum x6, other arithmetic, one_block(): jnp.sum(weight * (delta_w - radial * delta_z), axis=1)  8.98 us
    unnamed x18, local copies, waits for them, and re-layouts  4.55 us
  transfers between devices with their start and end apart: 2, of which 2 were waited for; matrix products, arithmetic and copies ran while one was open for 2% of the time, Pallas kernels for 0%

commit v1 on v0

v1 whole, which is shorter than its diff:
```python
import jax
import jax.numpy as jnp
from jax import lax
from jax.experimental import pallas as pl
from jax.experimental.pallas import tpu as pltpu
from jax.sharding import Mesh
from jax.sharding import PartitionSpec as P

Y, X, Z, REP = "blk_0", "blk_1", "blk_2", "rep"
BLK = (Y, X, Z)
FIELD_AXES = (Y, X)
ACT_AXIS = Z

STEP_TIME = 0.0625
SOFTEN_SQ = 0.0001
HALF_SQ = STEP_TIME * STEP_TIME / 2.0
LANES = 128
SLOTS = 16
WIDE = 256
LIMIT = 8 * 1024 * 1024
EXACT = lax.Precision.HIGHEST


def lane_iota(shape):
    return lax.broadcasted_iota(jnp.int32, shape, len(shape) - 1)


def row_iota(shape):
    return lax.broadcasted_iota(jnp.int32, shape, len(shape) - 2)


def tiled_slots(index_ref, scratch):
    scratch[...] = jnp.zeros(scratch.shape, jnp.int32)
    scratch[0:1, 0:SLOTS] = index_ref[...]
    row = scratch[0:1, :]
    for shift in (16, 32, 64):
        row = row + pltpu.roll(row, shift, 1)
    return row


def own_rows(shape):
    return row_iota(shape) == lane_iota(shape) // SLOTS


def prepare_kernel(pos, vel, acc, jerk, mass, index, field_out, act_out, state, slots):
    cubed = STEP_TIME * HALF_SQ / 3.0
    state[0:3, :] = pos[...] + STEP_TIME * vel[...] + HALF_SQ * acc[...] + cubed * jerk[...]
    state[3:6, :] = vel[...] + STEP_TIME * acc[...] + HALF_SQ * jerk[...]
    state[6:7, :] = mass[...]
    state[7:8, :] = jnp.zeros((1, state.shape[1]), jnp.float32)
    whole = state[...]
    half = jnp.where(lax.axis_index(REP) == 0, whole[:, :LANES], whole[:, LANES:])
    for k in range(field_out.shape[0]):
        field_out[k] = half
    shape = (whole.shape[1], LANES)
    chosen = (row_iota(shape) == tiled_slots(index, slots)).astype(jnp.float32)
    picked = jnp.dot(whole, chosen, precision=EXACT, preferred_element_type=jnp.float32)
    packed = jnp.sum(jnp.where(own_rows(picked.shape), picked, 0.0), axis=0, keepdims=True)
    for k in range(act_out.shape[0]):
        act_out[k] = packed


def line_base():
    y, x, z = lax.axis_index(Y), lax.axis_index(X), lax.axis_index(Z)
    return y, x, z


def forces_kernel(line, count, field, act, out, rows, active, sums):
    n_line = act.shape[0]
    n_field = field.shape[0]
    first, stride = line()
    rows[...] = jnp.zeros(rows.shape, jnp.float32)
    for k in range(n_line):
        rows[k : k + 1, :] = act[k]
    columns = rows[...].T
    starts = []
    lives = []
    total = 0
    for k in range(n_line):
        live = count[first + k * stride]
        starts.append(total)
        lives.append(live)
        total = total + live
    for k in range(n_line):
        spread = jnp.broadcast_to(columns[0:96, k : k + 1], (96, LANES))
        for c in range(6):
            active[c, pl.ds(starts[k], SLOTS), :] = spread[c * SLOTS : (c + 1) * SLOTS]

    def one_block(b, carry):
        at = pl.ds(pl.multiple_of(b * 8, 8), 8)
        mine = [active[c, at, :] for c in range(6)]

        def one_chunk(f, sums_here):
            def row(c):
                return jnp.broadcast_to(field[f, c : c + 1, :], (8, LANES))

            dx, dy, dz, du, dv, dw = [row(c) - mine[c] for c in range(6)]
            radius_sq = dx * dx + dy * dy + dz * dz + SOFTEN_SQ
            root = lax.rsqrt(radius_sq)
            inverse = root * root
            weight = row(6) * root * inverse
            radial = (dx * du + dy * dv + dz * dw) * inverse
            wx, wy, wz = weight * dx, weight * dy, weight * dz
            new = (wx, wy, wz, weight * du, weight * dv, weight * dw, radial * wx, radial * wy, radial * wz)
            return tuple(s + n for s, n in zip(sums_here, new))

        zero = jnp.zeros((8, LANES), jnp.float32)
        got = lax.fori_loop(0, n_field, one_chunk, (zero,) * 9, unroll=4)
        for c in range(3):
            sums[c, at, :] = got[c]
            sums[3 + c, at, :] = got[3 + c] - 3.0 * got[6 + c]
        return carry

    lax.fori_loop(0, (total + 7) // 8, one_block, 0)
    folded = jnp.zeros((8, WIDE), jnp.float32)
    for c in range(6):
        ones = (row_iota((8, LANES)) == c).astype(jnp.float32)
        row = lax.dot_general(
            ones, sums[c], (((1,), (1,)), ((), ())), precision=EXACT, preferred_element_type=jnp.float32
        )
        row = jnp.where(row_iota((8, WIDE)) == c, row, 0.0)
        folded = folded + (pltpu.roll(row, SLOTS * c, 1) if c else row)
    lane = lane_iota((8, LANES))
    owned = own_rows((8, LANES))
    for k in range(n_line):
        moved = (pltpu.roll(folded, WIDE - starts[k], 1) if k else folded)[:, :LANES]
        kept = jnp.where(owned & (lane % SLOTS < lives[k]), moved, 0.0)
        packed = jnp.sum(kept, axis=0, keepdims=True)
        out[2 * k] = packed
        out[2 * k + 1] = packed


def correct_kernel(count, parts, pos, vel, acc, jerk, index, new_pos, new_vel, new_acc, new_jerk, slots):
    y, x, z = line_base()
    live = count[(y * lax.axis_size(X) + x) * lax.axis_size(Z) + z]
    force = parts[0]
    for k in range(1, parts.shape[0]):
        force = force + parts[k]
    shape = (8, LANES)
    lane = lane_iota(shape)
    spread = jnp.where(own_rows(shape), jnp.broadcast_to(force, shape), 0.0)
    spread = jnp.where((row_iota(shape) == 6) & own_rows(shape), 1.0, spread)
    table = (pos.shape[1], LANES)
    chosen = (row_iota(table) == tiled_slots(index, slots)) & (lane_iota(table) % SLOTS < live)
    placed = lax.dot_general(
        spread, chosen.astype(jnp.float32), (((1,), (1,)), ((), ())), precision=EXACT, preferred_element_type=jnp.float32
    )
    hit = jnp.broadcast_to(placed[6:7], (3, placed.shape[1])) > 0.5
    acc_one, jerk_one = placed[0:3], placed[3:6]
    pos_zero, vel_zero, acc_zero, jerk_zero = pos[...], vel[...], acc[...], jerk[...]
    twelfth = STEP_TIME * STEP_TIME / 12.0
    vel_one = vel_zero + (acc_zero + acc_one) * (STEP_TIME / 2.0) + (jerk_zero - jerk_one) * twelfth
    pos_one = pos_zero + (vel_zero + vel_one) * (STEP_TIME / 2.0) + (acc_zero - acc_one) * twelfth
    new_pos[...] = jnp.where(hit, pos_one, pos_zero)
    new_vel[...] = jnp.where(hit, vel_one, vel_zero)
    new_acc[...] = jnp.where(hit, acc_one, acc_zero)
    new_jerk[...] = jnp.where(hit, jerk_one, jerk_zero)


def f32(*shape):
    return jax.ShapeDtypeStruct(shape, jnp.float32)


VMEM = pl.BlockSpec(memory_space=pltpu.VMEM)
SMEM = pl.BlockSpec(memory_space=pltpu.SMEM)


def shards(star_pos, star_vel, star_acc, star_jerk, masses, act_index, act_count):
    n_field = lax.axis_size(FIELD_AXES)
    n_line = lax.axis_size(ACT_AXIS)
    state = (star_pos, star_vel, star_acc, star_jerk)
    width = star_pos.shape[1]

    def line():
        y, x, z = line_base()
        return (y * lax.axis_size(X) + x) * lax.axis_size(Z), 1

    field, act = pl.pallas_call(
        prepare_kernel,
        out_shape=(f32(n_field, 8, LANES), f32(n_line, 1, LANES)),
        in_specs=[VMEM] * 6,
        out_specs=(VMEM, VMEM),
        scratch_shapes=[pltpu.VMEM((8, width), jnp.float32), pltpu.VMEM((8, LANES), jnp.int32)],
        compiler_params=pltpu.CompilerParams(vmem_limit_bytes=LIMIT),
        name="prepare",
    )(*state, masses[None, :], act_index)
    act = lax.all_to_all(act, ACT_AXIS, 0, 0, tiled=True)
    field = lax.all_to_all(field, FIELD_AXES, 0, 0, tiled=True)
    parts = pl.pallas_call(
        lambda *refs: forces_kernel(line, *refs),
        out_shape=f32(2 * n_line, 1, LANES),
        in_specs=[SMEM, VMEM, VMEM],
        out_specs=VMEM,
        scratch_shapes=[
            pltpu.VMEM((16, LANES), jnp.float32),
            pltpu.VMEM((6, WIDE, LANES), jnp.float32),
            pltpu.VMEM((6, WIDE, LANES), jnp.float32),
        ],
        compiler_params=pltpu.CompilerParams(vmem_limit_bytes=LIMIT),
        name="forces",
    )(act_count, field, act)
    parts = lax.all_to_all(parts, (ACT_AXIS, REP), 0, 0, tiled=True)
    return pl.pallas_call(
        correct_kernel,
        out_shape=tuple(f32(3, width) for _ in range(4)),
        in_specs=[SMEM] + [VMEM] * 6,
        out_specs=(VMEM,) * 4,
        scratch_shapes=[pltpu.VMEM((8, LANES), jnp.int32)],
        compiler_params=pltpu.CompilerParams(vmem_limit_bytes=LIMIT),
        name="correct",
    )(act_count, parts, *state, act_index)


def solution(mesh):
    finer = Mesh(mesh.devices.reshape(8, 4, 12, mesh.shape["rep"]), (Y, X, Z, REP))
    placed = (P(None, BLK), P(None, BLK), P(None, BLK), P(None, BLK), P(BLK), P(BLK, None), P())
    return jax.shard_map(
        shards,
        mesh=finer,
        in_specs=placed,
        out_specs=(P(None, BLK), P(None, BLK), P(None, BLK), P(None, BLK)),
        check_vma=False,
    )
```

time: 227 us -> 70.3 us (0.31)
  waiting for transfers between devices: 76.6 us -> 0 us
  blocking collectives: 110 us -> 59.3 us
  between operations: 14.9 us -> 0.71 us
  other arithmetic: 12.1 us -> 0 us
  local copies, waits for them, and re-layouts: 12.6 us -> 3.45 us
  Pallas kernels: 0 us -> 6.24 us
    reduce_scatter x2 -> x0, waiting for transfers between devices: 76.5 us -> none  [scatter_axes(): value = lax.psum_scatter(value, axis, scatter_dimension=dim, tiled=True)]
    all_gather x4 -> x0, blocking collectives: 75.8 us -> none  [the longest x3 61.1 us: gather_in_order(): tiles = lax.all_gather(tiles, axes[k])]
    all_to_all x0 -> x3, blocking collectives: none -> 59.3 us  [the longest x1 24.4 us: shards(): act = lax.all_to_all(act, ACT_AXIS, 0, 0, tiled=True)]
    unnamed x1 -> x0, blocking collectives: 34.5 us -> none
    reduce_sum x6 -> x0, other arithmetic: 8.98 us -> none  [one_block(): jnp.sum(weight * (delta_w - radial * delta_z), axis=1)]
    pallas_call x0 -> x3, Pallas kernels: none -> 6.24 us  [the longest x1 4.25 us: shards(): pl.pallas_call(lambda *refs: forces_kernel(line, *refs), out_shape=f32(2...]
    unnamed x18 -> x22, local copies, waits for them, and re-layouts: 4.55 us -> 3.45 us
  transfers between devices with their start and end apart: 2 -> 0, of which waited for: 2 -> 0; matrix products, arithmetic and copies ran while one was open for 2% -> 0% of each run, Pallas kernels for 0% -> 0%
where the time goes in v1:
time: 70.3 us; the launch traced here: 69.7 us
  blocking collectives  59.3 us (84%)
  Pallas kernels  6.24 us (9%)
  local copies, waits for them, and re-layouts  3.45 us (5%)
  between operations  0.71 us (1%)
    all_to_all x1, blocking collectives, shards(): act = lax.all_to_all(act, ACT_AXIS, 0, 0, tiled=True)  24.4 us
    all_to_all x1, blocking collectives, shards(): field = lax.all_to_all(field, FIELD_AXES, 0, 0, tiled=True)  18.9 us
    all_to_all x1, blocking collectives, shards(): parts = lax.all_to_all(parts, (ACT_AXIS, REP), 0, 0, tiled=True)  15.9 us
    pallas_call x1, Pallas kernels, shards(): pl.pallas_call(lambda *refs: forces_kernel(line, *refs), out_shape=f32(2...  4.25 us
    unnamed x22, local copies, waits for them, and re-layouts  3.45 us
    pallas_call x1, Pallas kernels, shards(): pl.pallas_call(correct_kernel, out_shape=tuple((f32(3, width) for _ in ra...  1.6 us

profile of v1, /device:TPU:1, one launch (start us, length us, event | category | flops | bytes accessed | tf_op | source)
XLA Modules:
  0.0 69.7 jit_solution(6528664771151452259)
XLA Ops:
  0.6 0.0 copy-start.9
  0.6 0.0 copy-start.10
  0.7 0.6 copy-done.9
  1.3 0.0 copy-done.10
  1.3 0.0 copy-start
  1.3 0.7 copy-done
  2.0 0.7 copy-done.2
  2.7 0.7 copy-done.4
  3.4 0.7 copy-done.6
  4.1 0.4 prepare.1
  4.5 24.4 %all_to_all.15.refs_2_ = f32[12,1,128]{2,1,0:T(1,128)S(1)} all-to-all(f32[12,1,128]{2,1,0:T(1,128)S(1)} %get-tuple-element.7), channel_id=1, replica_groups=mesh['blk_0'=8,'blk_1'=4,'blk_2'=12,'rep'=2] {'blk_2'}, dimensions={0} | all-to-all | bytes 12288 | tf_op jit(solution)/shard_map/all_to_all | solution.py:187
  28.9 18.9 %all_to_all.16.refs_1_ = f32[32,8,128]{2,1,0:T(8,128)S(1)} all-to-all(f32[32,8,128]{2,1,0:T(8,128)S(1)} %get-tuple-element.6), channel_id=1, replica_groups=mesh['blk_0'=8,'blk_1'=4,'blk_2'=12,'rep'=2] {'blk_0','blk_1'}, dimensions={0} | all-to-all | bytes 262144 | tf_op jit(solution)/shard_map/all_to_all | solution.py:188
  47.9 0.0 copy-done.8
  47.9 4.2 %forces.1 = f32[24,1,128]{2,1,0:T(1,128)S(1)} custom-call(s32[384]{0:T(512)S(1)} %copy-done.8, f32[32,8,128]{2,1,0:T(8,128)S(1)} %all_to_all.16.refs_1_, f32[12,1,128]{2,1,0:T(1,128)S(1)} %all_to_all.15.refs_2_), custom_call_target="tpu_custom_call" | custom-call | tf_op jit(solution)/shard_map/forces/pallas_call | solution.py:189
  52.1 0.0 copy-start.1
  52.1 0.0 copy-start.3
  52.1 0.0 copy-start.5
  52.1 0.0 copy-start.7
  52.2 15.9 %all_to_all.17.parts = f32[24,1,128]{2,1,0:T(1,128)S(1)} all-to-all(f32[24,1,128]{2,1,0:T(1,128)S(1)} %forces.1), channel_id=1, replica_groups=mesh['blk_0'=8,'blk_1'=4,'blk_2'=12,'rep'=2] {'blk_2','rep'}, dimensions={0} | all-to-all | bytes 24576 | tf_op jit(solution)/shard_map/all_to_all | solution.py:202
  68.1 0.0 copy-done.1
  68.1 0.0 copy-done.3
  68.1 0.0 copy-done.5
  68.1 0.0 copy-done.7
  68.1 1.6 %correct.1 = (f32[3,256]{1,0:T(4,128)}, f32[3,256]{1,0:T(4,128)}, f32[3,256]{1,0:T(4,128)}, f32[3,256]{1,0:T(4,128)}) custom-call(s32[384]{0:T(512)S(1)} %copy-done.8, f32[24,1,128]{2,1,0:T(1,128)S(1)} %all_to_all.17.parts, f32[3,256]{1,0:T(4,128)S(1)} %copy-done.1, f32[3,256]{1,0:T(4,128)S(1)} %copy-done.3, f32[3,256]{1,0:T(4,128)S(1)} %copy-done.5, ...), custom_call_target="tpu_custom_call" | custom-call | tf_op jit(solution)/shard_map/correct/pallas_call | solution.py:203
  (4 shorter events, 0.0 us)
Async XLA Ops:
  0.6 0.7 copy-start.9
  0.6 0.7 copy-start.10
  1.3 0.7 copy-start
  2.0 0.7 copy-start.2
  2.7 0.7 copy-start.4
  3.4 0.7 copy-start.6
  28.9 18.9 %copy-start.8 = (s32[384]{0:T(512)S(1)}, s32[384]{0:T(512)}, u32[]{:S(2)}) copy-start(s32[384]{0:T(512)} %count.1) | copy-start | bytes 4612
  52.1 16.0 %copy-start.1 = (f32[3,256]{1,0:T(4,128)S(1)}, f32[3,256]{1,0:T(4,128)}, u32[]{:S(2)}) copy-start(f32[3,256]{1,0:T(4,128)} %pos.3) | copy-start | bytes 9220
  52.1 16.0 %copy-start.3 = (f32[3,256]{1,0:T(4,128)S(1)}, f32[3,256]{1,0:T(4,128)}, u32[]{:S(2)}) copy-start(f32[3,256]{1,0:T(4,128)} %vel.3) | copy-start | bytes 9220
  52.1 16.0 %copy-start.5 = (f32[3,256]{1,0:T(4,128)S(1)}, f32[3,256]{1,0:T(4,128)}, u32[]{:S(2)}) copy-start(f32[3,256]{1,0:T(4,128)} %acc.3) | copy-start | bytes 9220
  52.1 16.0 %copy-start.7 = (f32[3,256]{1,0:T(4,128)S(1)}, f32[3,256]{1,0:T(4,128)}, u32[]{:S(2)}) copy-start(f32[3,256]{1,0:T(4,128)} %jerk.3) | copy-start | bytes 9220

commit v2 on v1

--- a/solution.py
+++ b/solution.py
@@ -8,8 +8,8 @@
 
 Y, X, Z, REP = "blk_0", "blk_1", "blk_2", "rep"
 BLK = (Y, X, Z)
-FIELD_AXES = (Y, X)
-ACT_AXIS = Z
+FIELD_AXES = (X, Z)
+ACT_AXIS = Y
 
 STEP_TIME = 0.0625
 SOFTEN_SQ = 0.0001
@@ -42,7 +42,16 @@
     return row_iota(shape) == lane_iota(shape) // SLOTS
 
 
-def prepare_kernel(pos, vel, acc, jerk, mass, index, field_out, act_out, state, slots):
+def prepare_kernel(*refs):
+    given, (field_out, act_out), (pos, vel, acc, jerk, mass, index, state, slots, done) = refs[:6], refs[6:8], refs[8:]
+    copies = [
+        pltpu.make_async_copy(far, near, done.at[k])
+        for k, (far, near) in enumerate(zip(given, (pos, vel, acc, jerk, mass, index)))
+    ]
+    for copy in copies:
+        copy.start()
+    for copy in copies:
+        copy.wait()
     cubed = STEP_TIME * HALF_SQ / 3.0
     state[0:3, :] = pos[...] + STEP_TIME * vel[...] + HALF_SQ * acc[...] + cubed * jerk[...]
     state[3:6, :] = vel[...] + STEP_TIME * acc[...] + HALF_SQ * jerk[...]
@@ -162,6 +171,7 @@
 
 
 VMEM = pl.BlockSpec(memory_space=pltpu.VMEM)
+HBM = pl.BlockSpec(memory_space=pltpu.HBM)
 SMEM = pl.BlockSpec(memory_space=pltpu.SMEM)
 
 
@@ -173,14 +183,21 @@
 
     def line():
         y, x, z = line_base()
-        return (y * lax.axis_size(X) + x) * lax.axis_size(Z), 1
+        return x * lax.axis_size(Z) + z, lax.axis_size(X) * lax.axis_size(Z)
 
     field, act = pl.pallas_call(
         prepare_kernel,
         out_shape=(f32(n_field, 8, LANES), f32(n_line, 1, LANES)),
-        in_specs=[VMEM] * 6,
+        in_specs=[HBM] * 6,
         out_specs=(VMEM, VMEM),
-        scratch_shapes=[pltpu.VMEM((8, width), jnp.float32), pltpu.VMEM((8, LANES), jnp.int32)],
+        scratch_shapes=[pltpu.VMEM((3, width), jnp.float32)] * 4
+        + [
+            pltpu.VMEM((1, width), jnp.float32),
+            pltpu.VMEM((1, SLOTS), jnp.int32),
+            pltpu.VMEM((8, width), jnp.float32),
+            pltpu.VMEM((8, LANES), jnp.int32),
+            pltpu.SemaphoreType.DMA((6,)),
+        ],
         compiler_params=pltpu.CompilerParams(vmem_limit_bytes=LIMIT),
         name="prepare",
     )(*state, masses[None, :], act_index)

time: 70.3 us -> 70.1 us (level)
  Pallas kernels: 6.24 us -> 7.11 us
    all_to_all x1, blocking collectives: 18.9 us -> 30.8 us  [shards(): field = lax.all_to_all(field, FIELD_AXES, 0, 0, tiled=True)]
    all_to_all x1, blocking collectives: 24.4 us -> 14 us  [shards(): act = lax.all_to_all(act, ACT_AXIS, 0, 0, tiled=True)]
    all_to_all x1, blocking collectives: 15.9 us -> 13.8 us  [shards(): parts = lax.all_to_all(parts, (ACT_AXIS, REP), 0, 0, tiled=True)]
    pallas_call x1, Pallas kernels: 4.25 us -> 5.03 us  [shards(): pl.pallas_call(lambda *refs: forces_kernel(line, *refs), out_shape=f32(2...]
where the time goes in v2:
time: 70.1 us; the launch traced here: 69.9 us
  blocking collectives  58.6 us (84%)
  Pallas kernels  7.11 us (10%)
  local copies, waits for them, and re-layouts  3.45 us (5%)
  between operations  0.71 us (1%)
    all_to_all x1, blocking collectives, shards(): field = lax.all_to_all(field, FIELD_AXES, 0, 0, tiled=True)  30.8 us
    all_to_all x1, blocking collectives, shards(): act = lax.all_to_all(act, ACT_AXIS, 0, 0, tiled=True)  14 us
    all_to_all x1, blocking collectives, shards(): parts = lax.all_to_all(parts, (ACT_AXIS, REP), 0, 0, tiled=True)  13.8 us
    pallas_call x1, Pallas kernels, shards(): pl.pallas_call(lambda *refs: forces_kernel(line, *refs), out_shape=f32(2...  5.03 us
    unnamed x22, local copies, waits for them, and re-layouts  3.45 us
    pallas_call x1, Pallas kernels, shards(): pl.pallas_call(correct_kernel, out_shape=tuple((f32(3, width) for _ in ra...  1.6 us

profile of v2, /device:TPU:1, one launch (start us, length us, event | category | flops | bytes accessed | tf_op | source)
XLA Modules:
  0.0 69.9 jit_solution(4654235934324099232)
XLA Ops:
  0.6 0.0 copy-start.9
  0.6 0.0 copy-start.10
  0.7 0.6 copy-done.9
  1.3 0.0 copy-done.10
  1.3 0.0 copy-start
  1.3 0.7 copy-done
  2.0 0.7 copy-done.2
  2.7 0.7 copy-done.4
  3.4 0.7 copy-done.6
  4.1 0.5 prepare.1
  4.6 14.0 %all_to_all.15.refs_2_ = f32[8,1,128]{2,1,0:T(1,128)S(1)} all-to-all(f32[8,1,128]{2,1,0:T(1,128)S(1)} %get-tuple-element.7), channel_id=1, replica_groups=mesh['blk_0'=8,'blk_1'=4,'blk_2'=12,'rep'=2] {'blk_0'}, dimensions={0} | all-to-all | bytes 8192 | tf_op jit(solution)/shard_map/all_to_all | solution.py:204
  18.6 30.8 %all_to_all.16.refs_1_ = f32[48,8,128]{2,1,0:T(8,128)S(1)} all-to-all(f32[48,8,128]{2,1,0:T(8,128)S(1)} %get-tuple-element.6), channel_id=1, replica_groups=mesh['blk_0'=8,'blk_1'=4,'blk_2'=12,'rep'=2] {'blk_1','blk_2'}, dimensions={0} | all-to-all | bytes 393216 | tf_op jit(solution)/shard_map/all_to_all | solution.py:205
  49.4 0.0 copy-done.8
  49.4 5.0 %forces.1 = f32[16,1,128]{2,1,0:T(1,128)S(1)} custom-call(s32[384]{0:T(512)S(1)} %copy-done.8, f32[48,8,128]{2,1,0:T(8,128)S(1)} %all_to_all.16.refs_1_, f32[8,1,128]{2,1,0:T(1,128)S(1)} %all_to_all.15.refs_2_), custom_call_target="tpu_custom_call" | custom-call | tf_op jit(solution)/shard_map/forces/pallas_call | solution.py:206
  54.4 0.0 copy-start.1
  54.4 0.0 copy-start.3
  54.4 0.0 copy-start.5
  54.5 0.0 copy-start.7
  54.5 13.8 %all_to_all.17.parts = f32[16,1,128]{2,1,0:T(1,128)S(1)} all-to-all(f32[16,1,128]{2,1,0:T(1,128)S(1)} %forces.1), channel_id=1, replica_groups=mesh['blk_0'=8,'blk_1'=4,'blk_2'=12,'rep'=2] {'blk_0','rep'}, dimensions={0} | all-to-all | bytes 16384 | tf_op jit(solution)/shard_map/all_to_all | solution.py:219
  68.3 0.0 copy-done.1
  68.3 0.0 copy-done.3
  68.3 0.0 copy-done.5
  68.3 0.0 copy-done.7
  68.3 1.6 %correct.1 = (f32[3,256]{1,0:T(4,128)}, f32[3,256]{1,0:T(4,128)}, f32[3,256]{1,0:T(4,128)}, f32[3,256]{1,0:T(4,128)}) custom-call(s32[384]{0:T(512)S(1)} %copy-done.8, f32[16,1,128]{2,1,0:T(1,128)S(1)} %all_to_all.17.parts, f32[3,256]{1,0:T(4,128)S(1)} %copy-done.1, f32[3,256]{1,0:T(4,128)S(1)} %copy-done.3, f32[3,256]{1,0:T(4,128)S(1)} %copy-done.5, ...), custom_call_target="tpu_custom_call" | custom-call | tf_op jit(solution)/shard_map/correct/pallas_call | solution.py:220
  (4 shorter events, 0.0 us)
Async XLA Ops:
  0.6 0.7 copy-start.9
  0.6 0.7 copy-start.10
  1.3 0.7 copy-start
  2.0 0.7 copy-start.2
  2.7 0.7 copy-start.4
  3.4 0.7 copy-start.6
  18.6 30.8 %copy-start.8 = (s32[384]{0:T(512)S(1)}, s32[384]{0:T(512)}, u32[]{:S(2)}) copy-start(s32[384]{0:T(512)} %count.1) | copy-start | bytes 4612
  54.4 13.9 %copy-start.1 = (f32[3,256]{1,0:T(4,128)S(1)}, f32[3,256]{1,0:T(4,128)}, u32[]{:S(2)}) copy-start(f32[3,256]{1,0:T(4,128)} %pos.1) | copy-start | bytes 9220
  54.4 13.8 %copy-start.3 = (f32[3,256]{1,0:T(4,128)S(1)}, f32[3,256]{1,0:T(4,128)}, u32[]{:S(2)}) copy-start(f32[3,256]{1,0:T(4,128)} %vel.1) | copy-start | bytes 9220
  54.4 13.8 %copy-start.5 = (f32[3,256]{1,0:T(4,128)S(1)}, f32[3,256]{1,0:T(4,128)}, u32[]{:S(2)}) copy-start(f32[3,256]{1,0:T(4,128)} %acc.1) | copy-start | bytes 9220
  54.5 13.8 %copy-start.7 = (f32[3,256]{1,0:T(4,128)S(1)}, f32[3,256]{1,0:T(4,128)}, u32[]{:S(2)}) copy-start(f32[3,256]{1,0:T(4,128)} %jerk.1) | copy-start | bytes 9220

commit v3 on v2

--- a/solution.py
+++ b/solution.py
@@ -65,8 +65,7 @@
     chosen = (row_iota(shape) == tiled_slots(index, slots)).astype(jnp.float32)
     picked = jnp.dot(whole, chosen, precision=EXACT, preferred_element_type=jnp.float32)
     packed = jnp.sum(jnp.where(own_rows(picked.shape), picked, 0.0), axis=0, keepdims=True)
-    for k in range(act_out.shape[0]):
-        act_out[k] = packed
+    act_out[...] = packed
 
 
 def line_base():
@@ -187,7 +186,7 @@
 
     field, act = pl.pallas_call(
         prepare_kernel,
-        out_shape=(f32(n_field, 8, LANES), f32(n_line, 1, LANES)),
+        out_shape=(pltpu.VMEM((n_field, 8, LANES), jnp.float32), pltpu.VMEM((1, LANES), jnp.float32)),
         in_specs=[HBM] * 6,
         out_specs=(VMEM, VMEM),
         scratch_shapes=[pltpu.VMEM((3, width), jnp.float32)] * 4
@@ -200,9 +199,9 @@
         ],
         compiler_params=pltpu.CompilerParams(vmem_limit_bytes=LIMIT),
         name="prepare",
-    )(*state, masses[None, :], act_index)
-    act = lax.all_to_all(act, ACT_AXIS, 0, 0, tiled=True)
+    )(*[pltpu.with_memory_space_constraint(a, pltpu.HBM) for a in (*state, masses[None, :], act_index)])
     field = lax.all_to_all(field, FIELD_AXES, 0, 0, tiled=True)
+    act = lax.all_gather(act, ACT_AXIS)
     parts = pl.pallas_call(
         lambda *refs: forces_kernel(line, *refs),
         out_shape=f32(2 * n_line, 1, LANES),

time: 70.1 us -> 58.6 us (0.84)
  blocking collectives: 58.6 us -> 30.7 us
  starting transfers between devices: 0 us -> 18.8 us
  local copies, waits for them, and re-layouts: 3.45 us -> 0.04 us
    all_to_all x2 -> x0, blocking collectives: 44.8 us -> none  [the longest x1 30.8 us: shards(): field = lax.all_to_all(field, FIELD_AXES, 0, 0, tiled=True)]
    all_to_all x0 -> x1, starting transfers between devices: none -> 18.8 us  [shards(): field = lax.all_to_all(field, FIELD_AXES, 0, 0, tiled=True)]
    all_gather x0 -> x1, blocking collectives: none -> 13.9 us  [shards(): act = lax.all_gather(act, ACT_AXIS)]
    unnamed x22 -> x12, local copies, waits for them, and re-layouts: 3.45 us -> 0.04 us
    all_to_all x1, blocking collectives: 13.8 us -> 16.8 us  [shards(): parts = lax.all_to_all(parts, (ACT_AXIS, REP), 0, 0, tiled=True)]
    pallas_call x1, Pallas kernels: 0.48 us -> 1.5 us  [shards(): pl.pallas_call(prepare_kernel, out_shape=(pltpu.VMEM((n_field, 8, LANES),...]
  transfers between devices with their start and end apart: 0 -> 1, of which waited for: 0 -> 0; matrix products, arithmetic and copies ran while one was open for 0% -> 0% of each run, Pallas kernels for 0% -> 0%
where the time goes in v3:
time: 58.6 us; the launch traced here: 58.1 us
  blocking collectives  30.7 us (52%)
  starting transfers between devices  18.8 us (32%)
  Pallas kernels  7.8 us (13%)
  between operations  0.71 us (1%)
    all_to_all x1, starting transfers between devices, shards(): field = lax.all_to_all(field, FIELD_AXES, 0, 0, tiled=True)  18.8 us
    all_to_all x1, blocking collectives, shards(): parts = lax.all_to_all(parts, (ACT_AXIS, REP), 0, 0, tiled=True)  16.8 us
    all_gather x1, blocking collectives, shards(): act = lax.all_gather(act, ACT_AXIS)  13.9 us
    pallas_call x1, Pallas kernels, shards(): pl.pallas_call(lambda *refs: forces_kernel(line, *refs), out_shape=f32(2...  4.7 us
    pallas_call x1, Pallas kernels, shards(): pl.pallas_call(correct_kernel, out_shape=tuple((f32(3, width) for _ in ra...  1.6 us
    pallas_call x1, Pallas kernels, shards(): pl.pallas_call(prepare_kernel, out_shape=(pltpu.VMEM((n_field, 8, LANES),...  1.5 us
  transfers between devices with their start and end apart: 1, of which 0 were waited for; matrix products, arithmetic and copies ran while one was open for 0% of the time, Pallas kernels for 0%

profile of v3, /device:TPU:1, one launch (start us, length us, event | category | flops | bytes accessed | tf_op | source)
XLA Modules:
  0.0 58.1 jit_solution(9954866224084641003)
XLA Ops:
  0.6 1.5 %prepare.1 = (f32[48,8,128]{2,1,0:T(8,128)}, f32[1,128]{1,0:T(1,128)S(1)}) custom-call(f32[3,256]{1,0:T(4,128)} %pos.1, f32[3,256]{1,0:T(4,128)} %vel.1, f32[3,256]{1,0:T(4,128)} %acc.1, f32[3,256]{1,0:T(4,128)} %jerk.1, f32[1,256]{1,0:T(1,128)} %bitcast.3, s32[1,16]{1,0:T(1,128)} %index.1), custom_call_target="tpu_custom_call" | custom-call | tf_op jit(solution)/shard_map/prepare/pallas_call | solution.py:187
  2.1 18.8 %all-to-all-start = ((f32[48,8,128]{2,1,0:T(8,128)}), f32[48,8,128]{2,1,0:T(8,128)S(1)}, u32[]{:S(2)}, u32[]{:S(2)}) async-start(f32[48,8,128]{2,1,0:T(8,128)} %get-tuple-element.6), calls=%async_computation | async-start | bytes 393216 | tf_op jit(solution)/shard_map/all_to_all | solution.py:203
  21.0 0.0 copy-start.4
  21.0 13.9 %all-gather.1.refs_2_ = f32[8,1,128]{2,1,0:T(1,128)S(1)} all-gather(f32[1,1,128]{2,1,0:T(1,128)S(1)} %bitcast.2), channel_id=2, replica_groups=mesh['blk_0'=8,'blk_1'=4,'blk_2'=12,'rep'=2] {'blk_0'}, dimensions={0}, use_global_device_ids=true | all-gather | bytes 4608 | tf_op jit(solution)/shard_map/all_gather | solution.py:204
  34.9 0.1 all-to-all-done.refs_1_
  34.9 0.0 copy-done.4
  34.9 0.0 copy-start.5
  34.9 4.7 %forces.1 = f32[16,1,128]{2,1,0:T(1,128)S(1)} custom-call(s32[384]{0:T(512)S(1)} %copy-done.4, f32[48,8,128]{2,1,0:T(8,128)S(1)} %all-to-all-done.refs_1_, f32[8,1,128]{2,1,0:T(1,128)S(1)} %all-gather.1.refs_2_), custom_call_target="tpu_custom_call" | custom-call | tf_op jit(solution)/shard_map/forces/pallas_call | solution.py:205
  39.6 0.0 copy-start
  39.7 0.0 copy-start.1
  39.7 0.0 copy-start.2
  39.7 0.0 copy-start.3
  39.7 16.8 %all_to_all.10.parts = f32[16,1,128]{2,1,0:T(1,128)S(1)} all-to-all(f32[16,1,128]{2,1,0:T(1,128)S(1)} %forces.1), channel_id=1, replica_groups=mesh['blk_0'=8,'blk_1'=4,'blk_2'=12,'rep'=2] {'blk_0','rep'}, dimensions={0} | all-to-all | bytes 16384 | tf_op jit(solution)/shard_map/all_to_all | solution.py:218
  56.5 0.0 copy-done.5
  56.5 0.0 copy-done
  56.5 0.0 copy-done.1
  56.5 0.0 copy-done.2
  56.5 0.0 copy-done.3
  56.5 1.6 %correct.1 = (f32[3,256]{1,0:T(4,128)}, f32[3,256]{1,0:T(4,128)}, f32[3,256]{1,0:T(4,128)}, f32[3,256]{1,0:T(4,128)}) custom-call(s32[384]{0:T(512)S(1)} %copy-done.4, f32[16,1,128]{2,1,0:T(1,128)S(1)} %all_to_all.10.parts, f32[3,256]{1,0:T(4,128)S(1)} %copy-done, f32[3,256]{1,0:T(4,128)S(1)} %copy-done.1, f32[3,256]{1,0:T(4,128)S(1)} %copy-done.2, ...), custom_call_target="tpu_custom_call" | custom-call | tf_op jit(solution)/shard_map/correct/pallas_call | solution.py:219
Async XLA Ops:
  2.1 32.8 %all-to-all-start = ((f32[48,8,128]{2,1,0:T(8,128)}), f32[48,8,128]{2,1,0:T(8,128)S(1)}, u32[]{:S(2)}, u32[]{:S(2)}) async-start(f32[48,8,128]{2,1,0:T(8,128)} %get-tuple-element.6), calls=%async_computation | async-start | bytes 393216 | tf_op jit(solution)/shard_map/all_to_all | solution.py:203
  21.0 13.9 %copy-start.4 = (s32[384]{0:T(512)S(1)}, s32[384]{0:T(512)}, u32[]{:S(2)}) copy-start(s32[384]{0:T(512)} %count.1) | copy-start | bytes 4612
  34.9 21.5 %copy-start.5 = (s32[1,16]{1,0:T(1,128)S(1)}, s32[1,16]{1,0:T(1,128)}, u32[]{:S(2)}) copy-start(s32[1,16]{1,0:T(1,128)} %index.1) | copy-start | bytes 196
  39.6 16.8 %copy-start = (f32[3,256]{1,0:T(4,128)S(1)}, f32[3,256]{1,0:T(4,128)}, u32[]{:S(2)}) copy-start(f32[3,256]{1,0:T(4,128)} %pos.1) | copy-start | bytes 9220
  39.7 16.8 %copy-start.1 = (f32[3,256]{1,0:T(4,128)S(1)}, f32[3,256]{1,0:T(4,128)}, u32[]{:S(2)}) copy-start(f32[3,256]{1,0:T(4,128)} %vel.1) | copy-start | bytes 9220
  39.7 16.8 %copy-start.2 = (f32[3,256]{1,0:T(4,128)S(1)}, f32[3,256]{1,0:T(4,128)}, u32[]{:S(2)}) copy-start(f32[3,256]{1,0:T(4,128)} %acc.1) | copy-start | bytes 9220
  39.7 16.8 %copy-start.3 = (f32[3,256]{1,0:T(4,128)S(1)}, f32[3,256]{1,0:T(4,128)}, u32[]{:S(2)}) copy-start(f32[3,256]{1,0:T(4,128)} %jerk.1) | copy-start | bytes 9220

commit v4 on v3

--- a/solution.py
+++ b/solution.py
@@ -16,9 +16,9 @@
 HALF_SQ = STEP_TIME * STEP_TIME / 2.0
 LANES = 128
 SLOTS = 16
-WIDE = 256
+WIDE = 128
 LIMIT = 8 * 1024 * 1024
-EXACT = lax.Precision.HIGHEST
+UNROLL = 12
 
 
 def lane_iota(shape):
@@ -62,8 +62,10 @@
     for k in range(field_out.shape[0]):
         field_out[k] = half
     shape = (whole.shape[1], LANES)
-    chosen = (row_iota(shape) == tiled_slots(index, slots)).astype(jnp.float32)
-    picked = jnp.dot(whole, chosen, precision=EXACT, preferred_element_type=jnp.float32)
+    chosen = (row_iota(shape) == tiled_slots(index, slots)).astype(jnp.bfloat16)
+    picked = jnp.zeros((8, LANES), jnp.float32)
+    for part in exact_parts(whole):
+        picked = picked + jnp.dot(part, chosen, preferred_element_type=jnp.float32)
     packed = jnp.sum(jnp.where(own_rows(picked.shape), picked, 0.0), axis=0, keepdims=True)
     act_out[...] = packed
 
@@ -73,26 +75,47 @@
     return y, x, z
 
 
-def forces_kernel(line, count, field, act, out, rows, active, sums):
+def exact_parts(value):
+    high = value.astype(jnp.bfloat16)
+    rest = value - high.astype(jnp.float32)
+    middle = rest.astype(jnp.bfloat16)
+    low = (rest - middle.astype(jnp.float32)).astype(jnp.bfloat16)
+    return high, middle, low
+
+
+def spread_kernel(line, count, index, act, active, meta, table, rows, slots):
+    y, x, z = line_base()
+    live = count[(y * lax.axis_size(X) + x) * lax.axis_size(Z) + z]
+    stars = jnp.broadcast_to(tiled_slots(index, slots), (8, LANES)).astype(jnp.float32).T[:, 0:1]
+    shape = (LANES, table.shape[1])
+    here = jnp.broadcast_to(stars, shape) == lane_iota(shape).astype(jnp.float32)
+    table[...] = (here & (row_iota(shape) % SLOTS < live)).astype(jnp.bfloat16)
     n_line = act.shape[0]
-    n_field = field.shape[0]
     first, stride = line()
     rows[...] = jnp.zeros(rows.shape, jnp.float32)
     for k in range(n_line):
         rows[k : k + 1, :] = act[k]
     columns = rows[...].T
-    starts = []
-    lives = []
-    total = 0
+    lane, row = lane_iota((8, LANES)), row_iota((8, LANES))
+    known = jnp.zeros((8, LANES), jnp.int32)
+    start = 0
     for k in range(n_line):
         live = count[first + k * stride]
-        starts.append(total)
-        lives.append(live)
-        total = total + live
-    for k in range(n_line):
+        known = jnp.where((row == 0) & (lane == k), start, known)
+        known = jnp.where((row == 1) & (lane == k), live, known)
         spread = jnp.broadcast_to(columns[0:96, k : k + 1], (96, LANES))
         for c in range(6):
-            active[c, pl.ds(starts[k], SLOTS), :] = spread[c * SLOTS : (c + 1) * SLOTS]
+            active[c, pl.ds(start, SLOTS), :] = spread[c * SLOTS : (c + 1) * SLOTS]
+        start = start + live
+    meta[...] = jnp.where(row == 2, start, known)
+
+
+def forces_kernel(meta, field, active, out, sums, known, done):
+    n_line = out.shape[0] // 2
+    n_field = field.shape[0]
+    copy = pltpu.make_async_copy(meta, known, done)
+    copy.start()
+    total = jnp.max(meta[2:3, :])
 
     def one_block(b, carry):
         at = pl.ds(pl.multiple_of(b * 8, 8), 8)
@@ -103,17 +126,17 @@
                 return jnp.broadcast_to(field[f, c : c + 1, :], (8, LANES))
 
             dx, dy, dz, du, dv, dw = [row(c) - mine[c] for c in range(6)]
-            radius_sq = dx * dx + dy * dy + dz * dz + SOFTEN_SQ
+            radius_sq = (dx * dx + dy * dy) + (dz * dz + SOFTEN_SQ)
             root = lax.rsqrt(radius_sq)
             inverse = root * root
-            weight = row(6) * root * inverse
+            weight = (row(6) * root) * inverse
             radial = (dx * du + dy * dv + dz * dw) * inverse
             wx, wy, wz = weight * dx, weight * dy, weight * dz
             new = (wx, wy, wz, weight * du, weight * dv, weight * dw, radial * wx, radial * wy, radial * wz)
             return tuple(s + n for s, n in zip(sums_here, new))
 
         zero = jnp.zeros((8, LANES), jnp.float32)
-        got = lax.fori_loop(0, n_field, one_chunk, (zero,) * 9, unroll=4)
+        got = lax.fori_loop(0, n_field, one_chunk, (zero,) * 9, unroll=UNROLL)
         for c in range(3):
             sums[c, at, :] = got[c]
             sums[3 + c, at, :] = got[3 + c] - 3.0 * got[6 + c]
@@ -122,37 +145,33 @@
     lax.fori_loop(0, (total + 7) // 8, one_block, 0)
     folded = jnp.zeros((8, WIDE), jnp.float32)
     for c in range(6):
-        ones = (row_iota((8, LANES)) == c).astype(jnp.float32)
-        row = lax.dot_general(
-            ones, sums[c], (((1,), (1,)), ((), ())), precision=EXACT, preferred_element_type=jnp.float32
-        )
+        ones = (row_iota((8, LANES)) == c).astype(jnp.bfloat16)
+        row = jnp.zeros((8, WIDE), jnp.float32)
+        for part in exact_parts(sums[c]):
+            row = row + lax.dot_general(ones, part, (((1,), (1,)), ((), ())), preferred_element_type=jnp.float32)
         row = jnp.where(row_iota((8, WIDE)) == c, row, 0.0)
         folded = folded + (pltpu.roll(row, SLOTS * c, 1) if c else row)
     lane = lane_iota((8, LANES))
     owned = own_rows((8, LANES))
+    copy.wait()
     for k in range(n_line):
-        moved = (pltpu.roll(folded, WIDE - starts[k], 1) if k else folded)[:, :LANES]
-        kept = jnp.where(owned & (lane % SLOTS < lives[k]), moved, 0.0)
+        moved = pltpu.roll(folded, WIDE - known[0, k], 1) if k else folded
+        kept = jnp.where(owned & (lane % SLOTS < known[1, k]), moved, 0.0)
         packed = jnp.sum(kept, axis=0, keepdims=True)
         out[2 * k] = packed
         out[2 * k + 1] = packed
 
 
-def correct_kernel(count, parts, pos, vel, acc, jerk, index, new_pos, new_vel, new_acc, new_jerk, slots):
-    y, x, z = line_base()
-    live = count[(y * lax.axis_size(X) + x) * lax.axis_size(Z) + z]
+def correct_kernel(table, parts, pos, vel, acc, jerk, new_pos, new_vel, new_acc, new_jerk):
     force = parts[0]
     for k in range(1, parts.shape[0]):
         force = force + parts[k]
     shape = (8, LANES)
-    lane = lane_iota(shape)
     spread = jnp.where(own_rows(shape), jnp.broadcast_to(force, shape), 0.0)
     spread = jnp.where((row_iota(shape) == 6) & own_rows(shape), 1.0, spread)
-    table = (pos.shape[1], LANES)
-    chosen = (row_iota(table) == tiled_slots(index, slots)) & (lane_iota(table) % SLOTS < live)
-    placed = lax.dot_general(
-        spread, chosen.astype(jnp.float32), (((1,), (1,)), ((), ())), precision=EXACT, preferred_element_type=jnp.float32
-    )
+    placed = jnp.zeros((8, table.shape[1]), jnp.float32)
+    for part in exact_parts(spread):
+        placed = placed + jnp.dot(part, table[...], preferred_element_type=jnp.float32)
     hit = jnp.broadcast_to(placed[6:7], (3, placed.shape[1])) > 0.5
     acc_one, jerk_one = placed[0:3], placed[3:6]
     pos_zero, vel_zero, acc_zero, jerk_zero = pos[...], vel[...], acc[...], jerk[...]
@@ -202,29 +221,38 @@
     )(*[pltpu.with_memory_space_constraint(a, pltpu.HBM) for a in (*state, masses[None, :], act_index)])
     field = lax.all_to_all(field, FIELD_AXES, 0, 0, tiled=True)
     act = lax.all_gather(act, ACT_AXIS)
+    call = dict(compiler_params=pltpu.CompilerParams(vmem_limit_bytes=LIMIT))
+    active, meta, table = pl.pallas_call(
+        lambda *refs: spread_kernel(line, *refs),
+        out_shape=(pltpu.VMEM((6, WIDE + SLOTS, LANES), jnp.float32), pltpu.VMEM((8, LANES), jnp.int32), pltpu.VMEM((LANES, width), jnp.bfloat16)),
+        in_specs=[SMEM, VMEM, VMEM],
+        out_specs=(VMEM,) * 3,
+        scratch_shapes=[pltpu.VMEM((8, LANES), jnp.float32), pltpu.VMEM((8, LANES), jnp.int32)],
+        name="spread",
+        **call,
+    )(act_count, act_index, act)
     parts = pl.pallas_call(
-        lambda *refs: forces_kernel(line, *refs),
-        out_shape=f32(2 * n_line, 1, LANES),
-        in_specs=[SMEM, VMEM, VMEM],
+        forces_kernel,
+        out_shape=pltpu.VMEM((2 * n_line, 1, LANES), jnp.float32),
+        in_specs=[VMEM] * 3,
         out_specs=VMEM,
         scratch_shapes=[
-            pltpu.VMEM((16, LANES), jnp.float32),
             pltpu.VMEM((6, WIDE, LANES), jnp.float32),
-            pltpu.VMEM((6, WIDE, LANES), jnp.float32),
+            pltpu.SMEM((8, LANES), jnp.int32),
+            pltpu.SemaphoreType.DMA(()),
         ],
-        compiler_params=pltpu.CompilerParams(vmem_limit_bytes=LIMIT),
         name="forces",
-    )(act_count, field, act)
+        **call,
+    )(meta, field, active)
     parts = lax.all_to_all(parts, (ACT_AXIS, REP), 0, 0, tiled=True)
     return pl.pallas_call(
         correct_kernel,
         out_shape=tuple(f32(3, width) for _ in range(4)),
-        in_specs=[SMEM] + [VMEM] * 6,
+        in_specs=[VMEM] * 6,
         out_specs=(VMEM,) * 4,
-        scratch_shapes=[pltpu.VMEM((8, LANES), jnp.int32)],
-        compiler_params=pltpu.CompilerParams(vmem_limit_bytes=LIMIT),
         name="correct",
-    )(act_count, parts, *state, act_index)
+        **call,
+    )(table, parts, *state)
 
 
 def solution(mesh):

time: 58.6 us -> 56.2 us (0.959)
  Pallas kernels: 7.8 us -> 6.31 us
  blocking collectives: 30.7 us -> 29.7 us
    all_to_all x1, blocking collectives: 16.8 us -> 15.8 us  [shards(): parts = lax.all_to_all(parts, (ACT_AXIS, REP), 0, 0, tiled=True)]
    pallas_call x1, Pallas kernels: 1.6 us -> 0.77 us  [shards(): pl.pallas_call(correct_kernel, out_shape=tuple((f32(3, width) for _ in ra...]
    pallas_call x1 -> x2, Pallas kernels: 4.7 us -> 4.03 us  [the longest x1 3.03 us: shards(): pl.pallas_call(forces_kernel, out_shape=pltpu.VMEM((2 * n_line, 1, LANES)...]
  transfers between devices with their start and end apart: 1 -> 1, of which waited for: 0 -> 0; matrix products, arithmetic and copies ran while one was open for 0% -> 0% of each run, Pallas kernels for 0% -> 2%
where the time goes in v4:
time: 56.2 us; the launch traced here: 55.6 us
  blocking collectives  29.7 us (53%)
  starting transfers between devices  18.8 us (33%)
  Pallas kernels  6.31 us (11%)
  between operations  0.73 us (1%)
    all_to_all x1, starting transfers between devices, shards(): field = lax.all_to_all(field, FIELD_AXES, 0, 0, tiled=True)  18.8 us
    all_to_all x1, blocking collectives, shards(): parts = lax.all_to_all(parts, (ACT_AXIS, REP), 0, 0, tiled=True)  15.8 us
    all_gather x1, blocking collectives, shards(): act = lax.all_gather(act, ACT_AXIS)  13.9 us
    pallas_call x1, Pallas kernels, shards(): pl.pallas_call(forces_kernel, out_shape=pltpu.VMEM((2 * n_line, 1, LANES)...  3.03 us
    pallas_call x1, Pallas kernels, shards(): pl.pallas_call(prepare_kernel, out_shape=(pltpu.VMEM((n_field, 8, LANES),...  1.5 us
  transfers between devices with their start and end apart: 1, of which 0 were waited for; matrix products, arithmetic and copies ran while one was open for 0% of the time, Pallas kernels for 2%

profile of v4, /device:TPU:1, one launch (start us, length us, event | category | flops | bytes accessed | tf_op | source)
XLA Modules:
  0.0 55.6 jit_solution(17854678850433146863)
XLA Ops:
  0.6 1.5 %prepare.1 = (f32[48,8,128]{2,1,0:T(8,128)}, f32[1,128]{1,0:T(1,128)S(1)}) custom-call(f32[3,256]{1,0:T(4,128)} %pos.1, f32[3,256]{1,0:T(4,128)} %vel.1, f32[3,256]{1,0:T(4,128)} %acc.1, f32[3,256]{1,0:T(4,128)} %jerk.1, f32[1,256]{1,0:T(1,128)} %bitcast.3, s32[1,16]{1,0:T(1,128)} %refs_1_.3), custom_call_target="tpu_custom_call" | custom-call | tf_op jit(solution)/shard_map/prepare/pallas_call | solution.py:206
  2.1 18.8 %all-to-all-start = ((f32[48,8,128]{2,1,0:T(8,128)}), f32[48,8,128]{2,1,0:T(8,128)S(1)}, u32[]{:S(2)}, u32[]{:S(2)}) async-start(f32[48,8,128]{2,1,0:T(8,128)} %get-tuple-element.12), calls=%async_computation | async-start | bytes 393216 | tf_op jit(solution)/shard_map/all_to_all | solution.py:222
  21.0 0.0 copy-start.4
  21.0 0.0 copy-start.5
  21.0 13.9 %all-gather.1.refs_2_ = f32[8,1,128]{2,1,0:T(1,128)S(1)} all-gather(f32[1,1,128]{2,1,0:T(1,128)S(1)} %bitcast.2), channel_id=2, replica_groups=mesh['blk_0'=8,'blk_1'=4,'blk_2'=12,'rep'=2] {'blk_0'}, dimensions={0}, use_global_device_ids=true | all-gather | bytes 4608 | tf_op jit(solution)/shard_map/all_gather | solution.py:223
  34.9 0.0 copy-done.4
  34.9 0.0 copy-done.5
  34.9 1.0 %spread.1 = (f32[6,144,128]{2,1,0:T(8,128)S(1)}, s32[8,128]{1,0:T(8,128)S(1)}, bf16[128,256]{1,0:T(8,128)(2,1)S(1)}) custom-call(s32[384]{0:T(512)S(1)} %copy-done.4, s32[1,16]{1,0:T(1,128)S(1)} %copy-done.5, f32[8,1,128]{2,1,0:T(1,128)S(1)} %all-gather.1.refs_2_), custom_call_target="tpu_custom_call" | custom-call | tf_op jit(solution)/shard_map/spread/pallas_call | solution.py:225
  35.9 0.0 all-to-all-done.field
  35.9 3.0 %forces.1 = f32[16,1,128]{2,1,0:T(1,128)S(1)} custom-call(s32[8,128]{1,0:T(8,128)S(1)} %get-tuple-element.11.meta, f32[48,8,128]{2,1,0:T(8,128)S(1)} %all-to-all-done.field, f32[6,144,128]{2,1,0:T(8,128)S(1)} %get-tuple-element.13.active), custom_call_target="tpu_custom_call" | custom-call | tf_op jit(solution)/shard_map/forces/pallas_call | solution.py:234
  39.0 0.0 copy-start
  39.0 0.0 copy-start.1
  39.0 0.0 copy-start.2
  39.0 0.0 copy-start.3
  39.0 15.8 %all_to_all.10.parts = f32[16,1,128]{2,1,0:T(1,128)S(1)} all-to-all(f32[16,1,128]{2,1,0:T(1,128)S(1)} %forces.1), channel_id=1, replica_groups=mesh['blk_0'=8,'blk_1'=4,'blk_2'=12,'rep'=2] {'blk_0','rep'}, dimensions={0} | all-to-all | bytes 16384 | tf_op jit(solution)/shard_map/all_to_all | solution.py:247
  54.8 0.0 copy-done
  54.8 0.0 copy-done.1
  54.8 0.0 copy-done.2
  54.8 0.0 copy-done.3
  54.8 0.8 %correct.1 = (f32[3,256]{1,0:T(4,128)}, f32[3,256]{1,0:T(4,128)}, f32[3,256]{1,0:T(4,128)}, f32[3,256]{1,0:T(4,128)}) custom-call(bf16[128,256]{1,0:T(8,128)(2,1)S(1)} %get-tuple-element.10.table, f32[16,1,128]{2,1,0:T(1,128)S(1)} %all_to_all.10.parts, f32[3,256]{1,0:T(4,128)S(1)} %copy-done, f32[3,256]{1,0:T(4,128)S(1)} %copy-done.1, ...), custom_call_target="tpu_custom_call" | custom-call | tf_op jit(solution)/shard_map/correct/pallas_call | solution.py:248
Async XLA Ops:
  2.1 33.8 %all-to-all-start = ((f32[48,8,128]{2,1,0:T(8,128)}), f32[48,8,128]{2,1,0:T(8,128)S(1)}, u32[]{:S(2)}, u32[]{:S(2)}) async-start(f32[48,8,128]{2,1,0:T(8,128)} %get-tuple-element.12), calls=%async_computation | async-start | bytes 393216 | tf_op jit(solution)/shard_map/all_to_all | solution.py:222
  21.0 13.9 %copy-start.4 = (s32[384]{0:T(512)S(1)}, s32[384]{0:T(512)}, u32[]{:S(2)}) copy-start(s32[384]{0:T(512)} %refs_0_.3) | copy-start | bytes 4612
  21.0 13.9 %copy-start.5 = (s32[1,16]{1,0:T(1,128)S(1)}, s32[1,16]{1,0:T(1,128)}, u32[]{:S(2)}) copy-start(s32[1,16]{1,0:T(1,128)} %refs_1_.3) | copy-start | bytes 196
  39.0 15.8 %copy-start = (f32[3,256]{1,0:T(4,128)S(1)}, f32[3,256]{1,0:T(4,128)}, u32[]{:S(2)}) copy-start(f32[3,256]{1,0:T(4,128)} %pos.1) | copy-start | bytes 9220
  39.0 15.8 %copy-start.1 = (f32[3,256]{1,0:T(4,128)S(1)}, f32[3,256]{1,0:T(4,128)}, u32[]{:S(2)}) copy-start(f32[3,256]{1,0:T(4,128)} %vel.1) | copy-start | bytes 9220
  39.0 15.8 %copy-start.2 = (f32[3,256]{1,0:T(4,128)S(1)}, f32[3,256]{1,0:T(4,128)}, u32[]{:S(2)}) copy-start(f32[3,256]{1,0:T(4,128)} %acc.1) | copy-start | bytes 9220
  39.0 15.8 %copy-start.3 = (f32[3,256]{1,0:T(4,128)S(1)}, f32[3,256]{1,0:T(4,128)}, u32[]{:S(2)}) copy-start(f32[3,256]{1,0:T(4,128)} %jerk.1) | copy-start | bytes 9220

commit v5 on v4

--- a/solution.py
+++ b/solution.py
@@ -42,11 +42,12 @@
     return row_iota(shape) == lane_iota(shape) // SLOTS
 
 
-def prepare_kernel(*refs):
-    given, (field_out, act_out), (pos, vel, acc, jerk, mass, index, state, slots, done) = refs[:6], refs[6:8], refs[8:]
+def prepare_kernel(line, *refs):
+    given, (field_out, act_out, meta, table) = refs[:7], refs[7:11]
+    pos, vel, acc, jerk, mass, index, count, state, slots, done = refs[11:]
     copies = [
         pltpu.make_async_copy(far, near, done.at[k])
-        for k, (far, near) in enumerate(zip(given, (pos, vel, acc, jerk, mass, index)))
+        for k, (far, near) in enumerate(zip(given, (pos, vel, acc, jerk, mass, index, count)))
     ]
     for copy in copies:
         copy.start()
@@ -62,12 +63,29 @@
     for k in range(field_out.shape[0]):
         field_out[k] = half
     shape = (whole.shape[1], LANES)
-    chosen = (row_iota(shape) == tiled_slots(index, slots)).astype(jnp.bfloat16)
+    tiled = tiled_slots(index, slots)
+    chosen = (row_iota(shape) == tiled).astype(jnp.bfloat16)
     picked = jnp.zeros((8, LANES), jnp.float32)
     for part in exact_parts(whole):
         picked = picked + jnp.dot(part, chosen, preferred_element_type=jnp.float32)
     packed = jnp.sum(jnp.where(own_rows(picked.shape), picked, 0.0), axis=0, keepdims=True)
     act_out[...] = packed
+    first, stride = line()
+    lane, row = lane_iota((8, LANES)), row_iota((8, LANES))
+    known = jnp.zeros((8, LANES), jnp.int32)
+    start = 0
+    for k in range(lax.axis_size(ACT_AXIS)):
+        live = count[first + k * stride]
+        known = jnp.where((row == 0) & (lane == k), start, known)
+        known = jnp.where((row == 1) & (lane == k), live, known)
+        start = start + live
+    meta[...] = jnp.where(row == 2, start, known)
+    y, x, z = line_base()
+    live = count[(y * lax.axis_size(X) + x) * lax.axis_size(Z) + z]
+    stars = jnp.broadcast_to(tiled, (8, LANES)).astype(jnp.float32).T[:, 0:1]
+    shape = (LANES, table.shape[1])
+    here = jnp.broadcast_to(stars, shape) == lane_iota(shape).astype(jnp.float32)
+    table[...] = (here & (row_iota(shape) % SLOTS < live)).astype(jnp.bfloat16)
 
 
 def line_base():
@@ -83,34 +101,21 @@
     return high, middle, low
 
 
-def spread_kernel(line, count, index, act, active, meta, table, rows, slots):
-    y, x, z = line_base()
-    live = count[(y * lax.axis_size(X) + x) * lax.axis_size(Z) + z]
-    stars = jnp.broadcast_to(tiled_slots(index, slots), (8, LANES)).astype(jnp.float32).T[:, 0:1]
-    shape = (LANES, table.shape[1])
-    here = jnp.broadcast_to(stars, shape) == lane_iota(shape).astype(jnp.float32)
-    table[...] = (here & (row_iota(shape) % SLOTS < live)).astype(jnp.bfloat16)
+def spread_kernel(meta, act, active, rows):
     n_line = act.shape[0]
-    first, stride = line()
     rows[...] = jnp.zeros(rows.shape, jnp.float32)
     for k in range(n_line):
         rows[k : k + 1, :] = act[k]
     columns = rows[...].T
-    lane, row = lane_iota((8, LANES)), row_iota((8, LANES))
-    known = jnp.zeros((8, LANES), jnp.int32)
-    start = 0
+    lane = lane_iota((1, LANES))
     for k in range(n_line):
-        live = count[first + k * stride]
-        known = jnp.where((row == 0) & (lane == k), start, known)
-        known = jnp.where((row == 1) & (lane == k), live, known)
+        start = jnp.max(jnp.where(lane == k, meta[0:1, :], 0)) if k else 0
         spread = jnp.broadcast_to(columns[0:96, k : k + 1], (96, LANES))
         for c in range(6):
             active[c, pl.ds(start, SLOTS), :] = spread[c * SLOTS : (c + 1) * SLOTS]
-        start = start + live
-    meta[...] = jnp.where(row == 2, start, known)
-
-
-def forces_kernel(meta, field, active, out, sums, known, done):
+
+
+def forces_kernel(order, meta, field, active, out, sums, known, done):
     n_line = out.shape[0] // 2
     n_field = field.shape[0]
     copy = pltpu.make_async_copy(meta, known, done)
@@ -158,8 +163,9 @@
         moved = pltpu.roll(folded, WIDE - known[0, k], 1) if k else folded
         kept = jnp.where(owned & (lane % SLOTS < known[1, k]), moved, 0.0)
         packed = jnp.sum(kept, axis=0, keepdims=True)
-        out[2 * k] = packed
-        out[2 * k + 1] = packed
+        for j, member in enumerate(order):
+            if member // 2 == k:
+                out[j] = packed
 
 
 def correct_kernel(table, parts, pos, vel, acc, jerk, new_pos, new_vel, new_acc, new_jerk):
@@ -190,7 +196,6 @@
 
 VMEM = pl.BlockSpec(memory_space=pltpu.VMEM)
 HBM = pl.BlockSpec(memory_space=pltpu.HBM)
-SMEM = pl.BlockSpec(memory_space=pltpu.SMEM)
 
 
 def shards(star_pos, star_vel, star_acc, star_jerk, masses, act_index, act_count):
@@ -203,36 +208,44 @@
         y, x, z = line_base()
         return x * lax.axis_size(Z) + z, lax.axis_size(X) * lax.axis_size(Z)
 
-    field, act = pl.pallas_call(
-        prepare_kernel,
-        out_shape=(pltpu.VMEM((n_field, 8, LANES), jnp.float32), pltpu.VMEM((1, LANES), jnp.float32)),
-        in_specs=[HBM] * 6,
-        out_specs=(VMEM, VMEM),
+    given = (*state, masses[None, :], act_index, act_count)
+    call = dict(compiler_params=pltpu.CompilerParams(vmem_limit_bytes=LIMIT))
+    field, act, meta, table = pl.pallas_call(
+        lambda *refs: prepare_kernel(line, *refs),
+        out_shape=(
+            pltpu.VMEM((n_field, 8, LANES), jnp.float32),
+            pltpu.VMEM((1, LANES), jnp.float32),
+            pltpu.VMEM((8, LANES), jnp.int32),
+            pltpu.VMEM((LANES, width), jnp.bfloat16),
+        ),
+        in_specs=[HBM] * 7,
+        out_specs=(VMEM,) * 4,
         scratch_shapes=[pltpu.VMEM((3, width), jnp.float32)] * 4
         + [
             pltpu.VMEM((1, width), jnp.float32),
             pltpu.VMEM((1, SLOTS), jnp.int32),
+            pltpu.SMEM(act_count.shape, jnp.int32),
             pltpu.VMEM((8, width), jnp.float32),
             pltpu.VMEM((8, LANES), jnp.int32),
-            pltpu.SemaphoreType.DMA((6,)),
+            pltpu.SemaphoreType.DMA((7,)),
         ],
-        compiler_params=pltpu.CompilerParams(vmem_limit_bytes=LIMIT),
         name="prepare",
-    )(*[pltpu.with_memory_space_constraint(a, pltpu.HBM) for a in (*state, masses[None, :], act_index)])
+        **call,
+    )(*[pltpu.with_memory_space_constraint(a, pltpu.HBM) for a in given])
     field = lax.all_to_all(field, FIELD_AXES, 0, 0, tiled=True)
     act = lax.all_gather(act, ACT_AXIS)
-    call = dict(compiler_params=pltpu.CompilerParams(vmem_limit_bytes=LIMIT))
-    active, meta, table = pl.pallas_call(
-        lambda *refs: spread_kernel(line, *refs),
-        out_shape=(pltpu.VMEM((6, WIDE + SLOTS, LANES), jnp.float32), pltpu.VMEM((8, LANES), jnp.int32), pltpu.VMEM((LANES, width), jnp.bfloat16)),
-        in_specs=[SMEM, VMEM, VMEM],
-        out_specs=(VMEM,) * 3,
-        scratch_shapes=[pltpu.VMEM((8, LANES), jnp.float32), pltpu.VMEM((8, LANES), jnp.int32)],
+    active = pl.pallas_call(
+        spread_kernel,
+        out_shape=pltpu.VMEM((6, WIDE + SLOTS, LANES), jnp.float32),
+        in_specs=[VMEM] * 2,
+        out_specs=VMEM,
+        scratch_shapes=[pltpu.VMEM((8, LANES), jnp.float32)],
         name="spread",
         **call,
-    )(act_count, act_index, act)
+    )(meta, act)
+    order = [2 * ((j // 2 + n_line // 2) % n_line) + 1 - j % 2 for j in range(2 * n_line)]
     parts = pl.pallas_call(
-        forces_kernel,
+        lambda *refs: forces_kernel(order, *refs),
         out_shape=pltpu.VMEM((2 * n_line, 1, LANES), jnp.float32),
         in_specs=[VMEM] * 3,
         out_specs=VMEM,
@@ -244,7 +257,7 @@
         name="forces",
         **call,
     )(meta, field, active)
-    parts = lax.all_to_all(parts, (ACT_AXIS, REP), 0, 0, tiled=True)
+    parts = lax.all_to_all(parts, (ACT_AXIS, REP), 0, 0, axis_index_groups=[order], tiled=True)
     return pl.pallas_call(
         correct_kernel,
         out_shape=tuple(f32(3, width) for _ in range(4)),

time: 56.2 us -> 53.3 us (0.948)
  blocking collectives: 29.7 us -> 26.3 us
  Pallas kernels: 6.31 us -> 7.33 us
    all_to_all x1, blocking collectives: 15.8 us -> 12.4 us  [shards(): lax.all_to_all(parts, (ACT_AXIS, REP), 0, 0, axis_index_groups=[order], t...]
    pallas_call x3, Pallas kernels: 5.54 us -> 6.56 us  [the longest x1 4.14 us: shards(): pl.pallas_call(lambda *refs: forces_kernel(order, *refs), out_shape=pltpu...]
  transfers between devices with their start and end apart: 1 -> 1, of which waited for: 0 -> 0; matrix products, arithmetic and copies ran while one was open for 0% -> 0% of each run, Pallas kernels for 2% -> 1%
where the time goes in v5:
time: 53.3 us; the launch traced here: 53.2 us
  blocking collectives  26.3 us (49%)
  starting transfers between devices  18.8 us (35%)
  Pallas kernels  7.33 us (14%)
  between operations  0.72 us (1%)
    all_to_all x1, starting transfers between devices, shards(): field = lax.all_to_all(field, FIELD_AXES, 0, 0, tiled=True)  18.8 us
    all_gather x1, blocking collectives, shards(): act = lax.all_gather(act, ACT_AXIS)  13.9 us
    all_to_all x1, blocking collectives, shards(): lax.all_to_all(parts, (ACT_AXIS, REP), 0, 0, axis_index_groups=[order], t...  12.4 us
    pallas_call x1, Pallas kernels, shards(): pl.pallas_call(lambda *refs: forces_kernel(order, *refs), out_shape=pltpu...  4.14 us
    pallas_call x1, Pallas kernels, shards(): pl.pallas_call(lambda *refs: prepare_kernel(line, *refs), out_shape=(pltp...  1.77 us
  transfers between devices with their start and end apart: 1, of which 0 were waited for; matrix products, arithmetic and copies ran while one was open for 0% of the time, Pallas kernels for 1%

profile of v5, /device:TPU:1, one launch (start us, length us, event | category | flops | bytes accessed | tf_op | source)
XLA Modules:
  0.0 53.2 jit_solution(583776053935304261)
XLA Ops:
  0.6 1.8 %prepare.1 = (f32[48,8,128]{2,1,0:T(8,128)}, f32[1,128]{1,0:T(1,128)S(1)}, s32[8,128]{1,0:T(8,128)S(1)}, bf16[128,256]{1,0:T(8,128)(2,1)S(1)}) custom-call(f32[3,256]{1,0:T(4,128)} %pos.1, f32[3,256]{1,0:T(4,128)} %vel.1, f32[3,256]{1,0:T(4,128)} %acc.1, f32[3,256]{1,0:T(4,128)} %jerk.1, f32[1,256]{1,0:T(1,128)} %bitcast.3, s32[1,16]{1,0:T(1,128)} %refs_5_.1, ...), custom_call_target="tpu_custom_call" | custom-call | tf_op jit(solution)/shard_map/prepare/pallas_call | solution.py:213
  2.4 18.8 %all-to-all-start = ((f32[48,8,128]{2,1,0:T(8,128)}), f32[48,8,128]{2,1,0:T(8,128)S(1)}, u32[]{:S(2)}, u32[]{:S(2)}) async-start(f32[48,8,128]{2,1,0:T(8,128)} %get-tuple-element.10), calls=%async_computation | async-start | bytes 393216 | tf_op jit(solution)/shard_map/all_to_all | solution.py:235
  21.3 13.9 %all-gather.1.act = f32[8,1,128]{2,1,0:T(1,128)S(1)} all-gather(f32[1,1,128]{2,1,0:T(1,128)S(1)} %bitcast.2), channel_id=2, replica_groups=mesh['blk_0'=8,'blk_1'=4,'blk_2'=12,'rep'=2] {'blk_0'}, dimensions={0}, use_global_device_ids=true | all-gather | bytes 4608 | tf_op jit(solution)/shard_map/all_gather | solution.py:236
  35.1 0.6 %spread.1.refs_2_ = f32[6,144,128]{2,1,0:T(8,128)S(1)} custom-call(s32[8,128]{1,0:T(8,128)S(1)} %get-tuple-element.9.meta.refs_0_, f32[8,1,128]{2,1,0:T(1,128)S(1)} %all-gather.1.act), custom_call_target="tpu_custom_call" | custom-call | tf_op jit(solution)/shard_map/spread/pallas_call | solution.py:237
  35.8 0.0 all-to-all-done.refs_1_
  35.8 4.1 %forces.1 = f32[16,1,128]{2,1,0:T(1,128)S(1)} custom-call(s32[8,128]{1,0:T(8,128)S(1)} %get-tuple-element.9.meta.refs_0_, f32[48,8,128]{2,1,0:T(8,128)S(1)} %all-to-all-done.refs_1_, f32[6,144,128]{2,1,0:T(8,128)S(1)} %spread.1.refs_2_), custom_call_target="tpu_custom_call" | custom-call | tf_op jit(solution)/shard_map/forces/pallas_call | solution.py:247
  40.0 0.0 copy-start
  40.0 0.0 copy-start.1
  40.0 0.0 copy-start.2
  40.0 0.0 copy-start.3
  40.0 12.4 %all_to_all.10.parts = f32[16,1,128]{2,1,0:T(1,128)S(1)} all-to-all(f32[16,1,128]{2,1,0:T(1,128)S(1)} %forces.1), channel_id=1, replica_groups={{385,384,481,480,577,576,673,672,1,0,97,96,193,192,289,288},{387,386,48..., dimensions={0} | all-to-all | bytes 16384 | tf_op jit(solution)/shard_map/all_to_all | solution.py:260
  52.4 0.0 copy-done
  52.4 0.0 copy-done.1
  52.4 0.0 copy-done.2
  52.4 0.0 copy-done.3
  52.4 0.8 %correct.1 = (f32[3,256]{1,0:T(4,128)}, f32[3,256]{1,0:T(4,128)}, f32[3,256]{1,0:T(4,128)}, f32[3,256]{1,0:T(4,128)}) custom-call(bf16[128,256]{1,0:T(8,128)(2,1)S(1)} %get-tuple-element.8.table, f32[16,1,128]{2,1,0:T(1,128)S(1)} %all_to_all.10.parts, f32[3,256]{1,0:T(4,128)S(1)} %copy-done, f32[3,256]{1,0:T(4,128)S(1)} %copy-done.1, ...), custom_call_target="tpu_custom_call" | custom-call | tf_op jit(solution)/shard_map/correct/pallas_call | solution.py:261
Async XLA Ops:
  2.4 33.4 %all-to-all-start = ((f32[48,8,128]{2,1,0:T(8,128)}), f32[48,8,128]{2,1,0:T(8,128)S(1)}, u32[]{:S(2)}, u32[]{:S(2)}) async-start(f32[48,8,128]{2,1,0:T(8,128)} %get-tuple-element.10), calls=%async_computation | async-start | bytes 393216 | tf_op jit(solution)/shard_map/all_to_all | solution.py:235
  40.0 12.5 %copy-start = (f32[3,256]{1,0:T(4,128)S(1)}, f32[3,256]{1,0:T(4,128)}, u32[]{:S(2)}) copy-start(f32[3,256]{1,0:T(4,128)} %pos.1) | copy-start | bytes 9220
  40.0 12.4 %copy-start.1 = (f32[3,256]{1,0:T(4,128)S(1)}, f32[3,256]{1,0:T(4,128)}, u32[]{:S(2)}) copy-start(f32[3,256]{1,0:T(4,128)} %vel.1) | copy-start | bytes 9220
  40.0 12.4 %copy-start.2 = (f32[3,256]{1,0:T(4,128)S(1)}, f32[3,256]{1,0:T(4,128)}, u32[]{:S(2)}) copy-start(f32[3,256]{1,0:T(4,128)} %acc.1) | copy-start | bytes 9220
  40.0 12.4 %copy-start.3 = (f32[3,256]{1,0:T(4,128)S(1)}, f32[3,256]{1,0:T(4,128)}, u32[]{:S(2)}) copy-start(f32[3,256]{1,0:T(4,128)} %jerk.1) | copy-start | bytes 9220

commit v6 on v5

--- a/solution.py
+++ b/solution.py
@@ -18,7 +18,7 @@
 SLOTS = 16
 WIDE = 128
 LIMIT = 8 * 1024 * 1024
-UNROLL = 12
+UNROLL = 24
 
 
 def lane_iota(shape):
@@ -44,14 +44,14 @@
 
 def prepare_kernel(line, *refs):
     given, (field_out, act_out, meta, table) = refs[:7], refs[7:11]
-    pos, vel, acc, jerk, mass, index, count, state, slots, done = refs[11:]
+    pos, vel, acc, jerk, mass, index, count, state, slots, tiles, done = refs[11:]
     copies = [
         pltpu.make_async_copy(far, near, done.at[k])
         for k, (far, near) in enumerate(zip(given, (pos, vel, acc, jerk, mass, index, count)))
     ]
     for copy in copies:
         copy.start()
-    for copy in copies:
+    for copy in copies[:5]:
         copy.wait()
     cubed = STEP_TIME * HALF_SQ / 3.0
     state[0:3, :] = pos[...] + STEP_TIME * vel[...] + HALF_SQ * acc[...] + cubed * jerk[...]
@@ -61,7 +61,10 @@
     whole = state[...]
     half = jnp.where(lax.axis_index(REP) == 0, whole[:, :LANES], whole[:, LANES:])
     for k in range(field_out.shape[0]):
-        field_out[k] = half
+        tiles[k] = half
+    sent = pltpu.make_async_copy(tiles, field_out, done.at[7])
+    sent.start()
+    copies[5].wait()
     shape = (whole.shape[1], LANES)
     tiled = tiled_slots(index, slots)
     chosen = (row_iota(shape) == tiled).astype(jnp.bfloat16)
@@ -70,6 +73,7 @@
         picked = picked + jnp.dot(part, chosen, preferred_element_type=jnp.float32)
     packed = jnp.sum(jnp.where(own_rows(picked.shape), picked, 0.0), axis=0, keepdims=True)
     act_out[...] = packed
+    copies[6].wait()
     first, stride = line()
     lane, row = lane_iota((8, LANES)), row_iota((8, LANES))
     known = jnp.zeros((8, LANES), jnp.int32)
@@ -86,6 +90,7 @@
     shape = (LANES, table.shape[1])
     here = jnp.broadcast_to(stars, shape) == lane_iota(shape).astype(jnp.float32)
     table[...] = (here & (row_iota(shape) % SLOTS < live)).astype(jnp.bfloat16)
+    sent.wait()
 
 
 def line_base():
@@ -213,13 +218,13 @@
     field, act, meta, table = pl.pallas_call(
         lambda *refs: prepare_kernel(line, *refs),
         out_shape=(
-            pltpu.VMEM((n_field, 8, LANES), jnp.float32),
+            pltpu.HBM((n_field, 8, LANES), jnp.float32),
             pltpu.VMEM((1, LANES), jnp.float32),
             pltpu.VMEM((8, LANES), jnp.int32),
             pltpu.VMEM((LANES, width), jnp.bfloat16),
         ),
         in_specs=[HBM] * 7,
-        out_specs=(VMEM,) * 4,
+        out_specs=(HBM, VMEM, VMEM, VMEM),
         scratch_shapes=[pltpu.VMEM((3, width), jnp.float32)] * 4
         + [
             pltpu.VMEM((1, width), jnp.float32),
@@ -227,7 +232,8 @@
             pltpu.SMEM(act_count.shape, jnp.int32),
             pltpu.VMEM((8, width), jnp.float32),
             pltpu.VMEM((8, LANES), jnp.int32),
-            pltpu.SemaphoreType.DMA((7,)),
+            pltpu.VMEM((n_field, 8, LANES), jnp.float32),
+            pltpu.SemaphoreType.DMA((8,)),
         ],
         name="prepare",
         **call,

time: 53.3 us -> 52 us (0.976); the launches traced: 53.2 us -> 50.9 us
  Pallas kernels: 7.33 us -> 5.08 us
    pallas_call x1, Pallas kernels: 4.14 us -> 2.15 us  [shards(): pl.pallas_call(lambda *refs: forces_kernel(order, *refs), out_shape=pltpu...]
where the time goes in v6:
time: 52 us; the launch traced here: 50.9 us
  blocking collectives  26.3 us (51%)
  starting transfers between devices  18.8 us (36%)
  Pallas kernels  5.08 us (10%)
  between operations  0.72 us (1%)
    all_to_all x1, starting transfers between devices, shards(): field = lax.all_to_all(field, FIELD_AXES, 0, 0, tiled=True)  18.8 us
    all_gather x1, blocking collectives, shards(): act = lax.all_gather(act, ACT_AXIS)  13.9 us
    all_to_all x1, blocking collectives, shards(): lax.all_to_all(parts, (ACT_AXIS, REP), 0, 0, axis_index_groups=[order], t...  12.4 us
    pallas_call x1, Pallas kernels, shards(): pl.pallas_call(lambda *refs: forces_kernel(order, *refs), out_shape=pltpu...  2.15 us
    pallas_call x1, Pallas kernels, shards(): pl.pallas_call(lambda *refs: prepare_kernel(line, *refs), out_shape=(pltp...  1.51 us
  transfers between devices with their start and end apart: 1, of which 0 were waited for; matrix products, arithmetic and copies ran while one was open for 0% of the time, Pallas kernels for 1%

profile of v6, /device:TPU:1, one launch (start us, length us, event | category | flops | bytes accessed | tf_op | source)
XLA Modules:
  0.0 50.9 jit_solution(6917001047097613258)
XLA Ops:
  0.6 1.5 %prepare.1 = (f32[48,8,128]{2,1,0:T(8,128)}, f32[1,128]{1,0:T(1,128)S(1)}, s32[8,128]{1,0:T(8,128)S(1)}, bf16[128,256]{1,0:T(8,128)(2,1)S(1)}) custom-call(f32[3,256]{1,0:T(4,128)} %pos.1, f32[3,256]{1,0:T(4,128)} %vel.1, f32[3,256]{1,0:T(4,128)} %acc.1, f32[3,256]{1,0:T(4,128)} %jerk.1, f32[1,256]{1,0:T(1,128)} %bitcast.3, s32[1,16]{1,0:T(1,128)} %refs_5_.1, ...), custom_call_target="tpu_custom_call" | custom-call | tf_op jit(solution)/shard_map/prepare/pallas_call | solution.py:218
  2.1 18.8 %all-to-all-start = ((f32[48,8,128]{2,1,0:T(8,128)}), f32[48,8,128]{2,1,0:T(8,128)S(1)}, u32[]{:S(2)}, u32[]{:S(2)}) async-start(f32[48,8,128]{2,1,0:T(8,128)} %get-tuple-element.10), calls=%async_computation | async-start | bytes 393216 | tf_op jit(solution)/shard_map/all_to_all | solution.py:241
  21.0 13.9 %all-gather.1.act = f32[8,1,128]{2,1,0:T(1,128)S(1)} all-gather(f32[1,1,128]{2,1,0:T(1,128)S(1)} %bitcast.2), channel_id=2, replica_groups=mesh['blk_0'=8,'blk_1'=4,'blk_2'=12,'rep'=2] {'blk_0'}, dimensions={0}, use_global_device_ids=true | all-gather | bytes 4608 | tf_op jit(solution)/shard_map/all_gather | solution.py:242
  34.9 0.6 %spread.1.refs_2_ = f32[6,144,128]{2,1,0:T(8,128)S(1)} custom-call(s32[8,128]{1,0:T(8,128)S(1)} %get-tuple-element.9.meta.refs_0_, f32[8,1,128]{2,1,0:T(1,128)S(1)} %all-gather.1.act), custom_call_target="tpu_custom_call" | custom-call | tf_op jit(solution)/shard_map/spread/pallas_call | solution.py:243
  35.5 0.0 all-to-all-done.refs_1_
  35.5 2.2 %forces.1 = f32[16,1,128]{2,1,0:T(1,128)S(1)} custom-call(s32[8,128]{1,0:T(8,128)S(1)} %get-tuple-element.9.meta.refs_0_, f32[48,8,128]{2,1,0:T(8,128)S(1)} %all-to-all-done.refs_1_, f32[6,144,128]{2,1,0:T(8,128)S(1)} %spread.1.refs_2_), custom_call_target="tpu_custom_call" | custom-call | tf_op jit(solution)/shard_map/forces/pallas_call | solution.py:253
  37.7 0.0 copy-start
  37.7 0.0 copy-start.1
  37.7 0.0 copy-start.2
  37.7 0.0 copy-start.3
  37.7 12.4 %all_to_all.10.parts = f32[16,1,128]{2,1,0:T(1,128)S(1)} all-to-all(f32[16,1,128]{2,1,0:T(1,128)S(1)} %forces.1), channel_id=1, replica_groups={{385,384,481,480,577,576,673,672,1,0,97,96,193,192,289,288},{387,386,48..., dimensions={0} | all-to-all | bytes 16384 | tf_op jit(solution)/shard_map/all_to_all | solution.py:266
  50.2 0.0 copy-done
  50.2 0.0 copy-done.1
  50.2 0.0 copy-done.2
  50.2 0.0 copy-done.3
  50.2 0.8 %correct.1 = (f32[3,256]{1,0:T(4,128)}, f32[3,256]{1,0:T(4,128)}, f32[3,256]{1,0:T(4,128)}, f32[3,256]{1,0:T(4,128)}) custom-call(bf16[128,256]{1,0:T(8,128)(2,1)S(1)} %get-tuple-element.8.table, f32[16,1,128]{2,1,0:T(1,128)S(1)} %all_to_all.10.parts, f32[3,256]{1,0:T(4,128)S(1)} %copy-done, f32[3,256]{1,0:T(4,128)S(1)} %copy-done.1, ...), custom_call_target="tpu_custom_call" | custom-call | tf_op jit(solution)/shard_map/correct/pallas_call | solution.py:267
Async XLA Ops:
  2.1 33.4 %all-to-all-start = ((f32[48,8,128]{2,1,0:T(8,128)}), f32[48,8,128]{2,1,0:T(8,128)S(1)}, u32[]{:S(2)}, u32[]{:S(2)}) async-start(f32[48,8,128]{2,1,0:T(8,128)} %get-tuple-element.10), calls=%async_computation | async-start | bytes 393216 | tf_op jit(solution)/shard_map/all_to_all | solution.py:241
  37.7 12.5 %copy-start = (f32[3,256]{1,0:T(4,128)S(1)}, f32[3,256]{1,0:T(4,128)}, u32[]{:S(2)}) copy-start(f32[3,256]{1,0:T(4,128)} %pos.1) | copy-start | bytes 9220
  37.7 12.4 %copy-start.1 = (f32[3,256]{1,0:T(4,128)S(1)}, f32[3,256]{1,0:T(4,128)}, u32[]{:S(2)}) copy-start(f32[3,256]{1,0:T(4,128)} %vel.1) | copy-start | bytes 9220
  37.7 12.4 %copy-start.2 = (f32[3,256]{1,0:T(4,128)S(1)}, f32[3,256]{1,0:T(4,128)}, u32[]{:S(2)}) copy-start(f32[3,256]{1,0:T(4,128)} %acc.1) | copy-start | bytes 9220
  37.7 12.4 %copy-start.3 = (f32[3,256]{1,0:T(4,128)S(1)}, f32[3,256]{1,0:T(4,128)}, u32[]{:S(2)}) copy-start(f32[3,256]{1,0:T(4,128)} %jerk.1) | copy-start | bytes 9220

commit v7 on v5

--- a/solution.py
+++ b/solution.py
@@ -18,7 +18,7 @@
 SLOTS = 16
 WIDE = 128
 LIMIT = 8 * 1024 * 1024
-UNROLL = 12
+UNROLL = 24
 
 
 def lane_iota(shape):

time: 53.3 us -> 52.7 us (0.989); the launches traced: 53.2 us -> 52 us
  Pallas kernels: 7.33 us -> 6.14 us
    pallas_call x1, Pallas kernels: 4.14 us -> 2.95 us  [shards(): pl.pallas_call(lambda *refs: forces_kernel(order, *refs), out_shape=pltpu...]
where the time goes in v7:
time: 52.7 us; the launch traced here: 52 us
  blocking collectives  26.3 us (50%)
  starting transfers between devices  18.8 us (36%)
  Pallas kernels  6.14 us (12%)
  between operations  0.72 us (1%)
    all_to_all x1, starting transfers between devices, shards(): field = lax.all_to_all(field, FIELD_AXES, 0, 0, tiled=True)  18.8 us
    all_gather x1, blocking collectives, shards(): act = lax.all_gather(act, ACT_AXIS)  13.9 us
    all_to_all x1, blocking collectives, shards(): lax.all_to_all(parts, (ACT_AXIS, REP), 0, 0, axis_index_groups=[order], t...  12.4 us
    pallas_call x1, Pallas kernels, shards(): pl.pallas_call(lambda *refs: forces_kernel(order, *refs), out_shape=pltpu...  2.95 us
    pallas_call x1, Pallas kernels, shards(): pl.pallas_call(lambda *refs: prepare_kernel(line, *refs), out_shape=(pltp...  1.77 us
  transfers between devices with their start and end apart: 1, of which 0 were waited for; matrix products, arithmetic and copies ran while one was open for 0% of the time, Pallas kernels for 1%

profile of v7, /device:TPU:1, one launch (start us, length us, event | category | flops | bytes accessed | tf_op | source)
XLA Modules:
  0.0 52.0 jit_solution(7072319540735233440)
XLA Ops:
  0.6 1.8 %prepare.1 = (f32[48,8,128]{2,1,0:T(8,128)}, f32[1,128]{1,0:T(1,128)S(1)}, s32[8,128]{1,0:T(8,128)S(1)}, bf16[128,256]{1,0:T(8,128)(2,1)S(1)}) custom-call(f32[3,256]{1,0:T(4,128)} %pos.1, f32[3,256]{1,0:T(4,128)} %vel.1, f32[3,256]{1,0:T(4,128)} %acc.1, f32[3,256]{1,0:T(4,128)} %jerk.1, f32[1,256]{1,0:T(1,128)} %bitcast.3, s32[1,16]{1,0:T(1,128)} %refs_5_.1, ...), custom_call_target="tpu_custom_call" | custom-call | tf_op jit(solution)/shard_map/prepare/pallas_call | solution.py:213
  2.4 18.8 %all-to-all-start = ((f32[48,8,128]{2,1,0:T(8,128)}), f32[48,8,128]{2,1,0:T(8,128)S(1)}, u32[]{:S(2)}, u32[]{:S(2)}) async-start(f32[48,8,128]{2,1,0:T(8,128)} %get-tuple-element.10), calls=%async_computation | async-start | bytes 393216 | tf_op jit(solution)/shard_map/all_to_all | solution.py:235
  21.3 13.9 %all-gather.1.act = f32[8,1,128]{2,1,0:T(1,128)S(1)} all-gather(f32[1,1,128]{2,1,0:T(1,128)S(1)} %bitcast.2), channel_id=2, replica_groups=mesh['blk_0'=8,'blk_1'=4,'blk_2'=12,'rep'=2] {'blk_0'}, dimensions={0}, use_global_device_ids=true | all-gather | bytes 4608 | tf_op jit(solution)/shard_map/all_gather | solution.py:236
  35.1 0.6 %spread.1.refs_2_ = f32[6,144,128]{2,1,0:T(8,128)S(1)} custom-call(s32[8,128]{1,0:T(8,128)S(1)} %get-tuple-element.9.meta.refs_0_, f32[8,1,128]{2,1,0:T(1,128)S(1)} %all-gather.1.act), custom_call_target="tpu_custom_call" | custom-call | tf_op jit(solution)/shard_map/spread/pallas_call | solution.py:237
  35.8 0.0 all-to-all-done.refs_1_
  35.8 3.0 %forces.1 = f32[16,1,128]{2,1,0:T(1,128)S(1)} custom-call(s32[8,128]{1,0:T(8,128)S(1)} %get-tuple-element.9.meta.refs_0_, f32[48,8,128]{2,1,0:T(8,128)S(1)} %all-to-all-done.refs_1_, f32[6,144,128]{2,1,0:T(8,128)S(1)} %spread.1.refs_2_), custom_call_target="tpu_custom_call" | custom-call | tf_op jit(solution)/shard_map/forces/pallas_call | solution.py:247
  38.8 0.0 copy-start
  38.8 0.0 copy-start.1
  38.8 0.0 copy-start.2
  38.8 0.0 copy-start.3
  38.8 12.4 %all_to_all.10.parts = f32[16,1,128]{2,1,0:T(1,128)S(1)} all-to-all(f32[16,1,128]{2,1,0:T(1,128)S(1)} %forces.1), channel_id=1, replica_groups={{385,384,481,480,577,576,673,672,1,0,97,96,193,192,289,288},{387,386,48..., dimensions={0} | all-to-all | bytes 16384 | tf_op jit(solution)/shard_map/all_to_all | solution.py:260
  51.2 0.0 copy-done
  51.2 0.0 copy-done.1
  51.2 0.0 copy-done.2
  51.2 0.0 copy-done.3
  51.2 0.8 %correct.1 = (f32[3,256]{1,0:T(4,128)}, f32[3,256]{1,0:T(4,128)}, f32[3,256]{1,0:T(4,128)}, f32[3,256]{1,0:T(4,128)}) custom-call(bf16[128,256]{1,0:T(8,128)(2,1)S(1)} %get-tuple-element.8.table, f32[16,1,128]{2,1,0:T(1,128)S(1)} %all_to_all.10.parts, f32[3,256]{1,0:T(4,128)S(1)} %copy-done, f32[3,256]{1,0:T(4,128)S(1)} %copy-done.1, ...), custom_call_target="tpu_custom_call" | custom-call | tf_op jit(solution)/shard_map/correct/pallas_call | solution.py:261
Async XLA Ops:
  2.4 33.4 %all-to-all-start = ((f32[48,8,128]{2,1,0:T(8,128)}), f32[48,8,128]{2,1,0:T(8,128)S(1)}, u32[]{:S(2)}, u32[]{:S(2)}) async-start(f32[48,8,128]{2,1,0:T(8,128)} %get-tuple-element.10), calls=%async_computation | async-start | bytes 393216 | tf_op jit(solution)/shard_map/all_to_all | solution.py:235
  38.8 12.5 %copy-start = (f32[3,256]{1,0:T(4,128)S(1)}, f32[3,256]{1,0:T(4,128)}, u32[]{:S(2)}) copy-start(f32[3,256]{1,0:T(4,128)} %pos.1) | copy-start | bytes 9220
  38.8 12.4 %copy-start.1 = (f32[3,256]{1,0:T(4,128)S(1)}, f32[3,256]{1,0:T(4,128)}, u32[]{:S(2)}) copy-start(f32[3,256]{1,0:T(4,128)} %vel.1) | copy-start | bytes 9220
  38.8 12.4 %copy-start.2 = (f32[3,256]{1,0:T(4,128)S(1)}, f32[3,256]{1,0:T(4,128)}, u32[]{:S(2)}) copy-start(f32[3,256]{1,0:T(4,128)} %acc.1) | copy-start | bytes 9220
  38.8 12.4 %copy-start.3 = (f32[3,256]{1,0:T(4,128)S(1)}, f32[3,256]{1,0:T(4,128)}, u32[]{:S(2)}) copy-start(f32[3,256]{1,0:T(4,128)} %jerk.1) | copy-start | bytes 9220

commit v8 on v7

--- a/solution.py
+++ b/solution.py
@@ -51,7 +51,7 @@
     ]
     for copy in copies:
         copy.start()
-    for copy in copies:
+    for copy in copies[:5]:
         copy.wait()
     cubed = STEP_TIME * HALF_SQ / 3.0
     state[0:3, :] = pos[...] + STEP_TIME * vel[...] + HALF_SQ * acc[...] + cubed * jerk[...]
@@ -63,6 +63,7 @@
     for k in range(field_out.shape[0]):
         field_out[k] = half
     shape = (whole.shape[1], LANES)
+    copies[5].wait()
     tiled = tiled_slots(index, slots)
     chosen = (row_iota(shape) == tiled).astype(jnp.bfloat16)
     picked = jnp.zeros((8, LANES), jnp.float32)
@@ -70,6 +71,7 @@
         picked = picked + jnp.dot(part, chosen, preferred_element_type=jnp.float32)
     packed = jnp.sum(jnp.where(own_rows(picked.shape), picked, 0.0), axis=0, keepdims=True)
     act_out[...] = packed
+    copies[6].wait()
     first, stride = line()
     lane, row = lane_iota((8, LANES)), row_iota((8, LANES))
     known = jnp.zeros((8, LANES), jnp.int32)

time: 52.7 us -> 52.9 us (level); the launches traced: 52 us -> 52.9 us
  Pallas kernels: 6.14 us -> 7.08 us
    pallas_call x1, Pallas kernels: 2.95 us -> 3.76 us  [shards(): pl.pallas_call(lambda *refs: forces_kernel(order, *refs), out_shape=pltpu...]
where the time goes in v8:
time: 52.9 us
  blocking collectives  26.3 us (50%)
  starting transfers between devices  18.8 us (36%)
  Pallas kernels  7.08 us (13%)
  between operations  0.72 us (1%)
    all_to_all x1, starting transfers between devices, shards(): field = lax.all_to_all(field, FIELD_AXES, 0, 0, tiled=True)  18.8 us
    all_gather x1, blocking collectives, shards(): act = lax.all_gather(act, ACT_AXIS)  13.9 us
    all_to_all x1, blocking collectives, shards(): lax.all_to_all(parts, (ACT_AXIS, REP), 0, 0, axis_index_groups=[order], t...  12.4 us
    pallas_call x1, Pallas kernels, shards(): pl.pallas_call(lambda *refs: forces_kernel(order, *refs), out_shape=pltpu...  3.76 us
    pallas_call x1, Pallas kernels, shards(): pl.pallas_call(lambda *refs: prepare_kernel(line, *refs), out_shape=(pltp...  1.9 us
  transfers between devices with their start and end apart: 1, of which 0 were waited for; matrix products, arithmetic and copies ran while one was open for 0% of the time, Pallas kernels for 1%

profile of v8, /device:TPU:1, one launch (start us, length us, event | category | flops | bytes accessed | tf_op | source)
XLA Modules:
  0.0 52.9 jit_solution(9351438071307363637)
XLA Ops:
  0.6 1.9 %prepare.1 = (f32[48,8,128]{2,1,0:T(8,128)}, f32[1,128]{1,0:T(1,128)S(1)}, s32[8,128]{1,0:T(8,128)S(1)}, bf16[128,256]{1,0:T(8,128)(2,1)S(1)}) custom-call(f32[3,256]{1,0:T(4,128)} %pos.1, f32[3,256]{1,0:T(4,128)} %vel.1, f32[3,256]{1,0:T(4,128)} %acc.1, f32[3,256]{1,0:T(4,128)} %jerk.1, f32[1,256]{1,0:T(1,128)} %bitcast.3, s32[1,16]{1,0:T(1,128)} %refs_5_.1, ...), custom_call_target="tpu_custom_call" | custom-call | tf_op jit(solution)/shard_map/prepare/pallas_call | solution.py:215
  2.5 18.8 %all-to-all-start = ((f32[48,8,128]{2,1,0:T(8,128)}), f32[48,8,128]{2,1,0:T(8,128)S(1)}, u32[]{:S(2)}, u32[]{:S(2)}) async-start(f32[48,8,128]{2,1,0:T(8,128)} %get-tuple-element.10), calls=%async_computation | async-start | bytes 393216 | tf_op jit(solution)/shard_map/all_to_all | solution.py:237
  21.4 13.9 %all-gather.1.act = f32[8,1,128]{2,1,0:T(1,128)S(1)} all-gather(f32[1,1,128]{2,1,0:T(1,128)S(1)} %bitcast.2), channel_id=2, replica_groups=mesh['blk_0'=8,'blk_1'=4,'blk_2'=12,'rep'=2] {'blk_0'}, dimensions={0}, use_global_device_ids=true | all-gather | bytes 4608 | tf_op jit(solution)/shard_map/all_gather | solution.py:238
  35.3 0.6 %spread.1.refs_2_ = f32[6,144,128]{2,1,0:T(8,128)S(1)} custom-call(s32[8,128]{1,0:T(8,128)S(1)} %get-tuple-element.9.meta.refs_0_, f32[8,1,128]{2,1,0:T(1,128)S(1)} %all-gather.1.act), custom_call_target="tpu_custom_call" | custom-call | tf_op jit(solution)/shard_map/spread/pallas_call | solution.py:239
  35.9 0.0 all-to-all-done.refs_1_
  35.9 3.8 %forces.1 = f32[16,1,128]{2,1,0:T(1,128)S(1)} custom-call(s32[8,128]{1,0:T(8,128)S(1)} %get-tuple-element.9.meta.refs_0_, f32[48,8,128]{2,1,0:T(8,128)S(1)} %all-to-all-done.refs_1_, f32[6,144,128]{2,1,0:T(8,128)S(1)} %spread.1.refs_2_), custom_call_target="tpu_custom_call" | custom-call | tf_op jit(solution)/shard_map/forces/pallas_call | solution.py:249
  39.7 0.0 copy-start
  39.7 0.0 copy-start.1
  39.7 0.0 copy-start.2
  39.7 0.0 copy-start.3
  39.8 12.4 %all_to_all.10.parts = f32[16,1,128]{2,1,0:T(1,128)S(1)} all-to-all(f32[16,1,128]{2,1,0:T(1,128)S(1)} %forces.1), channel_id=1, replica_groups={{385,384,481,480,577,576,673,672,1,0,97,96,193,192,289,288},{387,386,48..., dimensions={0} | all-to-all | bytes 16384 | tf_op jit(solution)/shard_map/all_to_all | solution.py:262
  52.2 0.0 copy-done
  52.2 0.0 copy-done.1
  52.2 0.0 copy-done.2
  52.2 0.0 copy-done.3
  52.2 0.8 %correct.1 = (f32[3,256]{1,0:T(4,128)}, f32[3,256]{1,0:T(4,128)}, f32[3,256]{1,0:T(4,128)}, f32[3,256]{1,0:T(4,128)}) custom-call(bf16[128,256]{1,0:T(8,128)(2,1)S(1)} %get-tuple-element.8.table, f32[16,1,128]{2,1,0:T(1,128)S(1)} %all_to_all.10.parts, f32[3,256]{1,0:T(4,128)S(1)} %copy-done, f32[3,256]{1,0:T(4,128)S(1)} %copy-done.1, ...), custom_call_target="tpu_custom_call" | custom-call | tf_op jit(solution)/shard_map/correct/pallas_call | solution.py:263
Async XLA Ops:
  2.5 33.4 %all-to-all-start = ((f32[48,8,128]{2,1,0:T(8,128)}), f32[48,8,128]{2,1,0:T(8,128)S(1)}, u32[]{:S(2)}, u32[]{:S(2)}) async-start(f32[48,8,128]{2,1,0:T(8,128)} %get-tuple-element.10), calls=%async_computation | async-start | bytes 393216 | tf_op jit(solution)/shard_map/all_to_all | solution.py:237
  39.7 12.5 %copy-start = (f32[3,256]{1,0:T(4,128)S(1)}, f32[3,256]{1,0:T(4,128)}, u32[]{:S(2)}) copy-start(f32[3,256]{1,0:T(4,128)} %pos.1) | copy-start | bytes 9220
  39.7 12.4 %copy-start.1 = (f32[3,256]{1,0:T(4,128)S(1)}, f32[3,256]{1,0:T(4,128)}, u32[]{:S(2)}) copy-start(f32[3,256]{1,0:T(4,128)} %vel.1) | copy-start | bytes 9220
  39.7 12.4 %copy-start.2 = (f32[3,256]{1,0:T(4,128)S(1)}, f32[3,256]{1,0:T(4,128)}, u32[]{:S(2)}) copy-start(f32[3,256]{1,0:T(4,128)} %acc.1) | copy-start | bytes 9220
  39.7 12.4 %copy-start.3 = (f32[3,256]{1,0:T(4,128)S(1)}, f32[3,256]{1,0:T(4,128)}, u32[]{:S(2)}) copy-start(f32[3,256]{1,0:T(4,128)} %jerk.1) | copy-start | bytes 9220

commit v9 on v8

--- a/solution.py
+++ b/solution.py
@@ -59,7 +59,7 @@
     state[6:7, :] = mass[...]
     state[7:8, :] = jnp.zeros((1, state.shape[1]), jnp.float32)
     whole = state[...]
-    half = jnp.where(lax.axis_index(REP) == 0, whole[:, :LANES], whole[:, LANES:])
+    half = jnp.where(lax.axis_index(REP) == 0, whole[:7, :LANES], whole[:7, LANES:])
     for k in range(field_out.shape[0]):
         field_out[k] = half
     shape = (whole.shape[1], LANES)
@@ -215,7 +215,7 @@
     field, act, meta, table = pl.pallas_call(
         lambda *refs: prepare_kernel(line, *refs),
         out_shape=(
-            pltpu.VMEM((n_field, 8, LANES), jnp.float32),
+            pltpu.VMEM((n_field, 7, LANES), jnp.float32),
             pltpu.VMEM((1, LANES), jnp.float32),
             pltpu.VMEM((8, LANES), jnp.int32),
             pltpu.VMEM((LANES, width), jnp.bfloat16),

time: 52.9 us -> 52.7 us (level)
  Pallas kernels: 7.08 us -> 6.54 us
    pallas_call x1, Pallas kernels: 3.76 us -> 3.22 us  [shards(): pl.pallas_call(lambda *refs: forces_kernel(order, *refs), out_shape=pltpu...]
where the time goes in v9:
time: 52.7 us; the launch traced here: 52.4 us
  blocking collectives  26.3 us (50%)
  starting transfers between devices  18.8 us (36%)
  Pallas kernels  6.54 us (12%)
  between operations  0.72 us (1%)
    all_to_all x1, starting transfers between devices, shards(): field = lax.all_to_all(field, FIELD_AXES, 0, 0, tiled=True)  18.8 us
    all_gather x1, blocking collectives, shards(): act = lax.all_gather(act, ACT_AXIS)  13.9 us
    all_to_all x1, blocking collectives, shards(): lax.all_to_all(parts, (ACT_AXIS, REP), 0, 0, axis_index_groups=[order], t...  12.4 us
    pallas_call x1, Pallas kernels, shards(): pl.pallas_call(lambda *refs: forces_kernel(order, *refs), out_shape=pltpu...  3.22 us
    pallas_call x1, Pallas kernels, shards(): pl.pallas_call(lambda *refs: prepare_kernel(line, *refs), out_shape=(pltp...  1.9 us
  transfers between devices with their start and end apart: 1, of which 0 were waited for; matrix products, arithmetic and copies ran while one was open for 0% of the time, Pallas kernels for 1%

profile of v9, /device:TPU:1, one launch (start us, length us, event | category | flops | bytes accessed | tf_op | source)
XLA Modules:
  0.0 52.4 jit_solution(6155469202193992274)
XLA Ops:
  0.6 1.9 %prepare.1 = (f32[48,7,128]{2,1,0:T(8,128)}, f32[1,128]{1,0:T(1,128)S(1)}, s32[8,128]{1,0:T(8,128)S(1)}, bf16[128,256]{1,0:T(8,128)(2,1)S(1)}) custom-call(f32[3,256]{1,0:T(4,128)} %pos.1, f32[3,256]{1,0:T(4,128)} %vel.1, f32[3,256]{1,0:T(4,128)} %acc.1, f32[3,256]{1,0:T(4,128)} %jerk.1, f32[1,256]{1,0:T(1,128)} %bitcast.3, s32[1,16]{1,0:T(1,128)} %refs_5_.1, ...), custom_call_target="tpu_custom_call" | custom-call | tf_op jit(solution)/shard_map/prepare/pallas_call | solution.py:215
  2.5 18.8 %all-to-all-start = ((f32[48,7,128]{2,1,0:T(8,128)}), f32[48,7,128]{2,1,0:T(8,128)S(1)}, u32[]{:S(2)}, u32[]{:S(2)}) async-start(f32[48,7,128]{2,1,0:T(8,128)} %get-tuple-element.10), calls=%async_computation | async-start | bytes 393216 | tf_op jit(solution)/shard_map/all_to_all | solution.py:237
  21.4 13.9 %all-gather.1.act = f32[8,1,128]{2,1,0:T(1,128)S(1)} all-gather(f32[1,1,128]{2,1,0:T(1,128)S(1)} %bitcast.2), channel_id=2, replica_groups=mesh['blk_0'=8,'blk_1'=4,'blk_2'=12,'rep'=2] {'blk_0'}, dimensions={0}, use_global_device_ids=true | all-gather | bytes 4608 | tf_op jit(solution)/shard_map/all_gather | solution.py:238
  35.3 0.6 %spread.1.refs_2_ = f32[6,144,128]{2,1,0:T(8,128)S(1)} custom-call(s32[8,128]{1,0:T(8,128)S(1)} %get-tuple-element.9.meta.refs_0_, f32[8,1,128]{2,1,0:T(1,128)S(1)} %all-gather.1.act), custom_call_target="tpu_custom_call" | custom-call | tf_op jit(solution)/shard_map/spread/pallas_call | solution.py:239
  35.9 0.0 all-to-all-done.refs_1_
  35.9 3.2 %forces.1 = f32[16,1,128]{2,1,0:T(1,128)S(1)} custom-call(s32[8,128]{1,0:T(8,128)S(1)} %get-tuple-element.9.meta.refs_0_, f32[48,7,128]{2,1,0:T(8,128)S(1)} %all-to-all-done.refs_1_, f32[6,144,128]{2,1,0:T(8,128)S(1)} %spread.1.refs_2_), custom_call_target="tpu_custom_call" | custom-call | tf_op jit(solution)/shard_map/forces/pallas_call | solution.py:249
  39.2 0.0 copy-start
  39.2 0.0 copy-start.1
  39.2 0.0 copy-start.2
  39.2 0.0 copy-start.3
  39.2 12.4 %all_to_all.10.parts = f32[16,1,128]{2,1,0:T(1,128)S(1)} all-to-all(f32[16,1,128]{2,1,0:T(1,128)S(1)} %forces.1), channel_id=1, replica_groups={{385,384,481,480,577,576,673,672,1,0,97,96,193,192,289,288},{387,386,48..., dimensions={0} | all-to-all | bytes 16384 | tf_op jit(solution)/shard_map/all_to_all | solution.py:262
  51.6 0.0 copy-done
  51.6 0.0 copy-done.1
  51.6 0.0 copy-done.2
  51.6 0.0 copy-done.3
  51.6 0.8 %correct.1 = (f32[3,256]{1,0:T(4,128)}, f32[3,256]{1,0:T(4,128)}, f32[3,256]{1,0:T(4,128)}, f32[3,256]{1,0:T(4,128)}) custom-call(bf16[128,256]{1,0:T(8,128)(2,1)S(1)} %get-tuple-element.8.table, f32[16,1,128]{2,1,0:T(1,128)S(1)} %all_to_all.10.parts, f32[3,256]{1,0:T(4,128)S(1)} %copy-done, f32[3,256]{1,0:T(4,128)S(1)} %copy-done.1, ...), custom_call_target="tpu_custom_call" | custom-call | tf_op jit(solution)/shard_map/correct/pallas_call | solution.py:263
Async XLA Ops:
  2.5 33.4 %all-to-all-start = ((f32[48,7,128]{2,1,0:T(8,128)}), f32[48,7,128]{2,1,0:T(8,128)S(1)}, u32[]{:S(2)}, u32[]{:S(2)}) async-start(f32[48,7,128]{2,1,0:T(8,128)} %get-tuple-element.10), calls=%async_computation | async-start | bytes 393216 | tf_op jit(solution)/shard_map/all_to_all | solution.py:237
  39.2 12.5 %copy-start = (f32[3,256]{1,0:T(4,128)S(1)}, f32[3,256]{1,0:T(4,128)}, u32[]{:S(2)}) copy-start(f32[3,256]{1,0:T(4,128)} %pos.1) | copy-start | bytes 9220
  39.2 12.4 %copy-start.1 = (f32[3,256]{1,0:T(4,128)S(1)}, f32[3,256]{1,0:T(4,128)}, u32[]{:S(2)}) copy-start(f32[3,256]{1,0:T(4,128)} %vel.1) | copy-start | bytes 9220
  39.2 12.4 %copy-start.2 = (f32[3,256]{1,0:T(4,128)S(1)}, f32[3,256]{1,0:T(4,128)}, u32[]{:S(2)}) copy-start(f32[3,256]{1,0:T(4,128)} %acc.1) | copy-start | bytes 9220
  39.2 12.4 %copy-start.3 = (f32[3,256]{1,0:T(4,128)S(1)}, f32[3,256]{1,0:T(4,128)}, u32[]{:S(2)}) copy-start(f32[3,256]{1,0:T(4,128)} %jerk.1) | copy-start | bytes 9220
